TPU v7x, 32 devices: a 4x4x1 block of a 4x4x8 slice. The times are simulated.
32 devices in a mesh: dp: 1 (over z), tp: 32 (over y, x, core).
Axes of the slice: x: 4, y: 4, z: 1, core: 2. Of those that a mesh axis runs over, the one named last changes fastest.
The devices are a block of a 4x4x8 slice.
Arguments:
- tokens: bfloat16 [1, 2048, 4096], P('dp', 'tp')
- doc_ids: int32 [1, 2048], P('dp', 'tp')
- norm1_gain: float32 [2, 4096], replicated
- norm1_shift: float32 [2, 4096], replicated
- qkv_weight: bfloat16 [2, 4096, 3, 32, 128], P(None, None, None, 'tp')
- out_weight: bfloat16 [2, 32, 128, 4096], P(None, 'tp')
- out_bias: float32 [2, 4096], replicated
- norm2_gain: float32 [2, 4096], replicated
- norm2_shift: float32 [2, 4096], replicated
- up_weight: bfloat16 [2, 4096, 16384], P(None, None, 'tp')
- up_bias: float32 [2, 16384], P(None, 'tp')
- down_weight: bfloat16 [2, 16384, 4096], P(None, 'tp')
- down_bias: float32 [2, 4096], replicated
Outputs:
- output: bfloat16 [1, 2048, 4096], P('dp', 'tp')
All inputs are finite; a program needn't handle non-finite values.
Results may differ from a plain program's by a relative error of at most 0.0120228.
Values are sent between devices in bfloat16 or wider.
A program may use at most 768 MiB of HBM per device.

v0:
```python
import functools
import math

import jax
import jax.numpy as jnp
from jax import lax
from jax.experimental import pallas as pl
from jax.experimental.pallas import tpu as pltpu
from jax.sharding import PartitionSpec as P

COLS = 512
MESH = pl.DeviceIdType.MESH
VMEM_LIMIT = 66 * 1000 * 1000

STEPS = (2, 1, -1, 0)
OTHER_SIDE = (2, -1, 1, 0)


class Place:
    def __init__(self, side):
        self.side = side
        self.me = lax.axis_index("tp")
        self.core = self.me % 2
        chip = self.me // 2
        self.x = chip % side
        self.y = chip // side
        self.partner = chip * 2 + 1 - self.core
        self.first = {1: self.dev(1, 0), -1: self.dev(-1, 0)}
        self.second = {1: self.dev(0, 1), -1: self.dev(0, -1)}

    def dev(self, i, j, core=None):
        core = self.core if core is None else core
        dx = i * (1 - core) + j * core
        dy = j * (1 - core) + i * core
        return (((self.y + dy + self.side) % self.side) * self.side + (self.x + dx + self.side) % self.side) * 2 + core

    def barrier(self):
        sem = pltpu.get_barrier_semaphore()
        others = [self.first[1], self.first[-1], self.second[1], self.second[-1], self.partner]
        for other in others:
            pl.semaphore_signal(sem, inc=1, device_id={"tp": other}, device_id_type=MESH)
        pl.semaphore_wait(sem, len(others))


def by_cols(width, fn):
    step = min(COLS, width)

    def body(n, carry):
        fn(pl.ds(pl.multiple_of(n * step, step), step))
        return carry

    lax.fori_loop(0, width // step, body, 0)


def scatter_kernel(side, layer, act_ref, w_hbm, res_ref, bias_ref, out_ref, w_ref, own, snd, prt, stg, mid, fin, stg2, mid2, fin2, w_sem, pair_send, pair_recv, send_sem, recv_sem):
    load_w = pltpu.make_async_copy(w_hbm.at[layer, 0] if len(w_hbm.shape) == 4 else w_hbm.at[layer], w_ref, w_sem)
    load_w.start()
    place = Place(side)
    rows, width = res_ref.shape
    half = rows // 2
    place.barrier()
    load_w.wait()

    def remote(src, dst, slot, device):
        return pltpu.make_async_remote_copy(src_ref=src, dst_ref=dst, send_sem=send_sem.at[slot], recv_sem=recv_sem.at[slot], device_id={"tp": device}, device_id_type=MESH)

    def pair_copy(g, jj):
        return pltpu.make_async_remote_copy(src_ref=snd.at[g % 2, jj], dst_ref=prt.at[g, jj], send_sem=pair_send.at[g, jj], recv_sem=pair_recv.at[g, jj], device_id={"tp": place.partner}, device_id_type=MESH)

    def product(core, g, dst):
        starts = [pl.multiple_of(place.dev(i, j, core) * rows + h * half, half) for j in STEPS for h, i in enumerate((STEPS[g], OTHER_SIDE[g]))]

        def piece(cols):
            lhs = jnp.concatenate([act_ref[pl.ds(s, half), :] for s in starts], axis=0)
            part = jnp.dot(lhs, w_ref[:, cols], preferred_element_type=jnp.float32).astype(jnp.bfloat16)
            for jj in range(side):
                dst[jj, :, cols] = part[jj * rows:(jj + 1) * rows]

        by_cols(width, piece)

    def pair_sum(g, jj, h, cols):
        at = pl.ds(h * half, half)
        return own[g, jj, at, cols].astype(jnp.float32) + prt[g, jj, at, cols].astype(jnp.float32)

    far, plus, minus, here = range(side)
    sent = []

    def send(src, dst, slot, device):
        copy = remote(src, dst, slot, device)
        copy.start()
        sent.append(copy)

    def arrived(dst, slot):
        remote(dst, dst, slot, place.me).wait_recv()

    def open_group(g):
        for jj in range(side):
            if g >= 2:
                pair_copy(g - 2, jj).wait_send()
        product(1 - place.core, g, snd.at[g % 2])
        for jj in range(side):
            pair_copy(g, jj).start()
        product(place.core, g, own.at[g])
        shared = set()
        for k, (jj, h) in enumerate(((far, 0), (far, 1), (plus, 1), (minus, 0))):
            if jj not in shared:
                shared.add(jj)
                pair_copy(g, jj).wait_recv()
            def stage(cols, k=k, jj=jj, h=h):
                stg[g, k, :, cols] = pair_sum(g, jj, h, cols)
            by_cols(width, stage)
            dst = mid.at[g, k] if k < 2 else fin.at[g, k]
            slot = 6 * g + (4 + k if k < 2 else k)
            send(stg.at[g, k], dst, slot, place.second[1 if k % 2 == 0 else -1])

    def relay(g):
        for k, (jj, h) in enumerate(((plus, 0), (minus, 1))):
            arrived(mid.at[g, k], 6 * g + 4 + k)
            def add(cols, k=k, jj=jj, h=h):
                mid[g, k, :, cols] += pair_sum(g, jj, h, cols)
            by_cols(width, add)
            send(mid.at[g, k], fin.at[g, k], 6 * g + k, place.second[1 if k == 0 else -1])

    base = 6 * side

    def close_group(g):
        pair_copy(g, here).wait_recv()
        for k in range(4):
            arrived(fin.at[g, k], 6 * g + k)

        def total(h, cols):
            return pair_sum(g, here, h, cols) + fin[g, 0 if h == 0 else 1, :, cols] + fin[g, 3 if h == 0 else 2, :, cols]

        def keep(k, h):
            def fn(cols):
                stg2[k, :, cols] = total(h, cols)
            by_cols(width, fn)

        def join(k):
            arrived(mid2.at[k], base + 4 + k)
            def fn(cols):
                mid2[k, :, cols] += total(k, cols)
            by_cols(width, fn)
            send(mid2.at[k], fin2.at[k], base + k, place.first[1 if k == 0 else -1])

        if g == far:
            keep(0, 0)
            send(stg2.at[0], mid2.at[0], base + 4, place.first[1])
            keep(1, 1)
            send(stg2.at[1], mid2.at[1], base + 5, place.first[-1])
        elif g == plus:
            join(0)
            join(1)
        elif g == minus:
            keep(2, 1)
            send(stg2.at[2], fin2.at[2], base + 2, place.first[1])
            keep(3, 0)
            send(stg2.at[3], fin2.at[3], base + 3, place.first[-1])
        else:
            for k in range(4):
                arrived(fin2.at[k], base + k)
            for h in range(2):
                def fn(cols, h=h):
                    at = pl.ds(h * half, half)
                    summed = total(h, cols) + fin2[0 if h == 0 else 1, :, cols] + fin2[3 if h == 0 else 2, :, cols]
                    out_ref[at, cols] = res_ref[at, cols] + (summed + bias_ref[layer:layer + 1, cols])
                by_cols(width, fn)

    open_group(0)
    open_group(1)
    open_group(2)
    relay(0)
    open_group(3)
    relay(1)
    close_group(0)
    relay(2)
    close_group(1)
    relay(3)
    close_group(2)
    close_group(3)
    for g in (side - 2, side - 1):
        for jj in range(side):
            pair_copy(g, jj).wait_send()
    for copy in sent:
        copy.wait_send()


def project_and_scatter(side, call_id, layer, act, weight, residual, bias):
    rows, width = residual.shape
    depth = act.shape[1]
    half = rows // 2
    quad = (side, side, rows, width)
    part = (side, 2, half, width)
    vmem = pl.BlockSpec(memory_space=pltpu.VMEM)
    return pl.pallas_call(
        functools.partial(scatter_kernel, side, layer),
        out_shape=jax.ShapeDtypeStruct((rows, width), jnp.float32),
        in_specs=[vmem, pl.BlockSpec(memory_space=pl.ANY), vmem, vmem],
        out_specs=vmem,
        scratch_shapes=[
            pltpu.VMEM((depth, width), jnp.bfloat16),
            pltpu.VMEM(quad, jnp.bfloat16),
            pltpu.VMEM((2,) + quad[1:], jnp.bfloat16),
            pltpu.VMEM(quad, jnp.bfloat16),
            pltpu.VMEM((side, 4, half, width), jnp.float32),
            pltpu.VMEM(part, jnp.float32),
            pltpu.VMEM((side, 4, half, width), jnp.float32),
            pltpu.VMEM((4, half, width), jnp.float32),
            pltpu.VMEM((2, half, width), jnp.float32),
            pltpu.VMEM((4, half, width), jnp.float32),
            pltpu.SemaphoreType.DMA,
            pltpu.SemaphoreType.DMA((side, side)),
            pltpu.SemaphoreType.DMA((side, side)),
            pltpu.SemaphoreType.DMA((6 * side + 6,)),
            pltpu.SemaphoreType.DMA((6 * side + 6,)),
        ],
        compiler_params=pltpu.CompilerParams(collective_id=call_id, has_side_effects=True, vmem_limit_bytes=VMEM_LIMIT),
        name=f"scatter_{call_id}",
    )(act, weight, residual, bias)


GATHER_ORDER = sorted(((i, j) for i in STEPS for j in STEPS), key=lambda at: (2 * abs(at[0]) + 3 * abs(at[1]), at))


def gather_kernel(side, layer, gelu, tail, res_ref, gain_ref, shift_ref, w_hbm, b_ref, *refs):
    tails, refs = (refs[0], refs[1:]) if tail else (None, refs)
    out, refs = refs[0], refs[1:]
    tails_out, refs = (refs[0], refs[1:]) if tail else (None, refs)
    (w_ref, buf, w_sem, send_sem, recv_sem, pair_send, pair_recv) = refs
    if len(w_hbm.shape) == 3:
        loads = [pltpu.make_async_copy(w_hbm.at[layer], w_ref, w_sem.at[0])]
    else:
        each = w_hbm.shape[4]
        loads = [pltpu.make_async_copy(w_hbm.at[layer, k, 0], w_ref.at[:, pl.ds(k * each, each)], w_sem.at[k]) for k in range(w_hbm.shape[1])]
    for load in loads:
        load.start()
    place = Place(side)
    rows, width = res_ref.shape
    half = rows // 2
    for at in (pl.ds(0, half), pl.ds(half, half)):
        residual = res_ref[at, :]
        centered = residual - jnp.mean(residual, axis=-1, keepdims=True)
        variance = jnp.mean(centered * centered, axis=-1, keepdims=True)
        normed = centered * lax.rsqrt(variance + 1e-5) * gain_ref[layer:layer + 1, :] + shift_ref[layer:layer + 1, :]
        buf[place.me, at, pl.ds(0, width)] = normed.astype(jnp.bfloat16)
    if tail:
        buf[place.me, :, pl.ds(width, tail)] = tails[...]
    place.barrier()

    def view(i, j, h, core=None):
        return buf.at[place.dev(i, j, core), pl.ds(h * half, half)]

    def wrap(k):
        return (k + 1) % side - 1

    def slot(i, j, h):
        return ((i % side) * side + j % side) * 2 + h

    sent = []

    def send(i, j, h, axis, step):
        there = (wrap(i - step), j) if axis == 0 else (i, wrap(j - step))
        device = (place.first, place.second)[axis][step]
        index = slot(i, j, h)
        copy = pltpu.make_async_remote_copy(src_ref=view(i, j, h), dst_ref=view(i, j, h), send_sem=send_sem.at[axis * 2 + (step > 0), index], recv_sem=recv_sem.at[slot(*there, h)], device_id={"tp": device}, device_id_type=MESH)
        copy.start()
        sent.append(copy)

    def pair(i, j, h, core=None):
        index = slot(i, j, h)
        ref = view(i, j, h, core)
        return pltpu.make_async_remote_copy(src_ref=ref, dst_ref=ref, send_sem=pair_send.at[index], recv_sem=pair_recv.at[index], device_id={"tp": place.partner}, device_id_type=MESH)

    def share(i, j, h):
        copy = pair(i, j, h)
        copy.start()
        sent.append(copy)

    def arrived(i, j, h):
        ref = view(i, j, h)
        pltpu.make_async_remote_copy(src_ref=ref, dst_ref=ref, send_sem=send_sem.at[0, 0], recv_sem=recv_sem.at[slot(i, j, h)], device_id={"tp": place.me}, device_id_type=MESH).wait_recv()

    def multiply(shards, core):
        devs = [place.dev(i, j, core) for i, j in shards]
        wide = w_ref.shape[1]
        step = wide if wide % 256 else 256
        at = [pl.ds(pl.multiple_of(d * rows, rows), rows) for d in devs]
        if tail:
            for d, where in zip(devs, at):
                tails_out[where, :] = buf[d, :, pl.ds(width, tail)]

        def piece(cols):
            lhs = jnp.concatenate([buf[d, :, pl.ds(0, width)] for d in devs], axis=0)
            part = jnp.dot(lhs, w_ref[:, cols], preferred_element_type=jnp.float32)
            if gelu:
                part = jax.nn.gelu(part + b_ref[layer:layer + 1, cols], approximate=True)
            part = part.astype(jnp.bfloat16)
            for k, where in enumerate(at):
                out[where, cols] = part[k * rows:(k + 1) * rows]

        if step == wide:
            piece(pl.ds(0, wide))
        else:
            def body(n, carry):
                piece(pl.ds(pl.multiple_of(n * step, step), step))
                return carry
            lax.fori_loop(0, wide // step, body, 0)

    def forward(i, j, h):
        if j == 0:
            if i == 0:
                send(i, j, h, 0, 1)
                send(i, j, h, 0, -1)
            elif i == -1 and h == 0:
                send(i, j, h, 0, 1)
            elif i == 1 and h == 1:
                send(i, j, h, 0, -1)
            send(i, j, h, 1, 1)
            send(i, j, h, 1, -1)
        elif j == -1 and h == 0:
            send(i, j, h, 1, 1)
        elif j == 1 and h == 1:
            send(i, j, h, 1, -1)
        share(i, j, h)

    for h in range(2):
        forward(0, 0, h)
    for load in loads:
        load.wait()
    cuts = (0, 4, 8, 12, 14, 16)
    for start, stop in zip(cuts, cuts[1:]):
        shards = GATHER_ORDER[start:stop]
        lead = [(i, j, 1 if 1 in (i, j) and -1 not in (i, j) else 0) for i, j in shards if (i, j) != (0, 0)]
        for i, j, h in lead + [(i, j, 1 - h) for i, j, h in lead]:
            arrived(i, j, h)
            forward(i, j, h)
        for i, j in shards:
            for h in range(2):
                pair(i, j, h, 1 - place.core).wait_recv()

        def both(k, carry):
            multiply(shards, (place.core + k) % 2)
            return carry

        lax.fori_loop(0, 2, both, 0)
    for copy in sent:
        copy.wait_send()


def gather_and_project(side, call_id, layer, residual, gain, shift, weight, bias, gelu, tails=None):
    rows, width = residual.shape
    tail = 0 if tails is None else tails.shape[1]
    extra = [] if tails is None else [tails]
    groups = 2 * side * side
    wide = weight.shape[2] if weight.ndim == 3 else weight.shape[1] * weight.shape[4]
    vmem = pl.BlockSpec(memory_space=pltpu.VMEM)
    outs = pl.pallas_call(
        functools.partial(gather_kernel, side, layer, gelu, tail),
        out_shape=[jax.ShapeDtypeStruct((groups * rows, wide), jnp.bfloat16)] + [jax.ShapeDtypeStruct((groups * rows, tail), jnp.bfloat16) for _ in extra],
        in_specs=[vmem, vmem, vmem, pl.BlockSpec(memory_space=pl.ANY), vmem] + [vmem for _ in extra],
        out_specs=[vmem] * (1 + len(extra)),
        scratch_shapes=[
            pltpu.VMEM((width, wide), jnp.bfloat16),
            pltpu.VMEM((groups, rows, width + tail), jnp.bfloat16),
            pltpu.SemaphoreType.DMA((3,)),
            pltpu.SemaphoreType.DMA((4, groups)),
            pltpu.SemaphoreType.DMA((groups,)),
            pltpu.SemaphoreType.DMA((groups,)),
            pltpu.SemaphoreType.DMA((groups,)),
        ],
        compiler_params=pltpu.CompilerParams(collective_id=call_id, has_side_effects=True, vmem_limit_bytes=VMEM_LIMIT),
        name=f"gather_{call_id}",
    )(residual, gain, shift, weight, bias, *extra)
    return outs if len(outs) > 1 else outs[0]


QUERY_BLOCK = 256
RING = ((-1, 0), (1, 1), (-1, 1), (1, 0), (2, 0), (2, 1))


def attend_kernel(side, layer, qkv_ref, ids_ref, row_ids_ref, w_hbm, res_ref, bias_ref, out_ref, w_own, wbuf, obuf, o_own, scores, acc, rbuf, load_sem, ws_send, ws_recv, wg_send, wg_recv, os_send, os_recv, og_send, og_recv, op_send, op_recv, back_send, back_recv):
    load_w = pltpu.make_async_copy(w_hbm.at[layer, 0], w_own, load_sem)
    load_w.start()
    me = lax.axis_index("tp")
    core = me % 2
    x = me // 2 % side
    y = me // 2 // side
    rows, width = res_ref.shape
    dim = w_own.shape[0]
    share = width // (2 * side)
    parts, _, _, cols = wbuf.shape
    line = rows * 2 * side
    steps = STEPS

    def at(dx, dy, dc):
        return (((y + dy + side) % side) * side + (x + dx + side) % side) * 2 + (core + dc) % 2

    peers = [at(dx, 0, dc) for dx in steps for dc in (1, 0) if (dx, dc) != (0, 0)]
    columns = [at(0, dy, 0) for dy in steps[:3]]
    barrier = pltpu.get_barrier_semaphore()
    for peer in peers + columns:
        pl.semaphore_signal(barrier, inc=1, device_id={"tp": peer}, device_id_type=MESH)
    pl.semaphore_wait(barrier, len(peers) + len(columns))
    load_w.wait()

    sent = []

    def send(src, dst, send_sem, recv_sem, device):
        if device is None:
            copy = pltpu.make_async_copy(src, dst, recv_sem)
        else:
            copy = pltpu.make_async_remote_copy(src_ref=src, dst_ref=dst, send_sem=send_sem, recv_sem=recv_sem, device_id={"tp": device}, device_id_type=MESH)
            sent.append(copy)
        copy.start()

    def arrived(dst, recv_sem):
        pltpu.make_async_copy(dst, dst, recv_sem).wait()

    def target(dx, dy, dc):
        return None if (dx, dy, dc) == (0, 0, 0) else at(dx, dy, dc)

    def first_col(device, part):
        return pl.multiple_of(device % (2 * side) * share + part * cols, 128)

    for part in range(parts):
        for k, dx in enumerate(steps):
            for dc in range(2):
                src = w_own.at[:, pl.ds(first_col(at(dx, 0, dc), part), cols)]
                send(src, wbuf.at[part, me], ws_send.at[part, k, dc], ws_recv.at[part, k, dc], target(dx, 0, dc))

    def w_slots(part, j, h):
        return wbuf.at[part, pl.ds(((y + j + side) % side) * 2 * side + h * side, side)]

    def w_ring(part, j, h):
        index = RING.index((j, h))
        return wg_send.at[part, index], wg_recv.at[part, index]

    def w_first(part):
        for k, dx in enumerate(steps):
            for dc in range(2):
                arrived(wbuf.at[part, at(-dx, 0, dc)], ws_recv.at[part, k, dc])
        for h in range(2):
            send(w_slots(part, 0, h), w_slots(part, 0, h), *w_ring(part, -1, h), at(0, 1, 0))
            send(w_slots(part, 0, 1 - h), w_slots(part, 0, 1 - h), *w_ring(part, 1, 1 - h), at(0, -1, 0))

    def w_arrived(part, j, h):
        arrived(w_slots(part, j, h), w_ring(part, j, h)[1])

    def w_relay(part):
        w_arrived(part, -1, 0)
        send(w_slots(part, -1, 0), w_slots(part, -1, 0), *w_ring(part, 2, 0), at(0, 1, 0))
        w_arrived(part, 1, 1)
        send(w_slots(part, 1, 1), w_slots(part, 1, 1), *w_ring(part, 2, 1), at(0, -1, 0))

    block = scores.shape[0]
    half = block // 2

    def attend(b):
        q_rows = pl.ds(pl.multiple_of(b * block, block), block)
        q = qkv_ref[q_rows, pl.ds(0, dim)]
        q_ids = ids_ref[q_rows, 0:1].astype(jnp.float32)
        q_pos = b * block + lax.broadcasted_iota(jnp.int32, (block, block), 0)

        def chunk(c):
            return pl.ds(pl.multiple_of(c * block, block), block)

        def score(c, top):
            s = lax.dot_general(q, qkv_ref[chunk(c), pl.ds(dim, dim)], (((1,), (1,)), ((), ())), preferred_element_type=jnp.float32) * dim ** -0.5
            k_pos = c * block + lax.broadcasted_iota(jnp.int32, (block, block), 1)
            allowed = (k_pos <= q_pos) & (row_ids_ref[0:1, chunk(c)] == q_ids)
            s = jnp.where(allowed, s, -1e30)
            scores[:, chunk(c)] = s
            return jnp.maximum(top, jnp.maximum(s[:, :half], s[:, half:]))

        top = jnp.max(lax.fori_loop(0, b + 1, score, jnp.full((block, half), -1e30, jnp.float32)), axis=-1, keepdims=True)

        def power(c, total):
            e = jnp.exp(scores[:, chunk(c)] - top)
            scores[:, chunk(c)] = e
            return total + (e[:, :half] + e[:, half:])

        total = jnp.sum(lax.fori_loop(0, b + 1, power, jnp.zeros((block, half), jnp.float32)), axis=-1, keepdims=True)
        inverse = 1.0 / total

        def mix(c, mixed):
            probs = (scores[:, chunk(c)] * inverse).astype(jnp.bfloat16)
            return mixed + jnp.dot(probs, qkv_ref[chunk(c), pl.ds(2 * dim, dim)], preferred_element_type=jnp.float32)

        o_own[q_rows, :] = lax.fori_loop(0, b + 1, mix, jnp.zeros((block, dim), jnp.float32)).astype(jnp.bfloat16)

    def o_slot(c, xx, yy):
        return (c * side + xx) * side + yy

    def attend_line(k):
        n = (y + steps[k] + side) % side

        def body(b, carry):
            attend(n * (line // block) + b)
            return carry

        lax.fori_loop(0, line // block, body, 0)
        src = o_own.at[pl.ds(pl.multiple_of(n * line, line), line)]
        send(src, obuf.at[o_slot(core, x, y)], os_send.at[k], os_recv.at[k], target(0, steps[k], 0))

    def o_slots(i, h, dc=0):
        return obuf.at[pl.ds(o_slot((core + dc) % 2, (x + i + side) % side, h * (side // 2)), side // 2)]

    def o_send(i, h, step, index):
        send(o_slots(i, h), o_slots(i, h), og_send.at[index], og_recv.at[index], at(step, 0, 0))

    def o_share(k, i, h):
        send(o_slots(i, h), o_slots(i, h), op_send.at[k], op_recv.at[k], at(0, 0, 1))

    attend_line(0)
    attend_line(1)
    w_first(0)
    attend_line(2)
    w_first(1)
    attend_line(3)
    w_relay(0)
    for k, dy in enumerate(steps):
        arrived(obuf.at[o_slot(core, x, (y - dy + side) % side)], os_recv.at[k])
    for h in range(2):
        o_send(0, h, 1, RING.index((-1, h)))
        o_send(0, 1 - h, -1, RING.index((1, 1 - h)))
    w_first(2)
    for h in range(2):
        o_share(h, 0, h)
    w_relay(1)
    w_first(3)
    for k, (i, h) in enumerate(RING):
        arrived(o_slots(i, h), og_recv.at[k])
        if (i, h) == (-1, 0):
            o_send(i, h, 1, RING.index((2, 0)))
        if (i, h) == (1, 1):
            o_send(i, h, -1, RING.index((2, 1)))
        o_share(2 + k, i, h)
        if k == 3:
            w_relay(2)
    for k, (i, h) in enumerate(((0, 0), (0, 1)) + RING):
        arrived(o_slots(i, h, 1), op_recv.at[k])

    strip = min(block, line)

    def project(part, j):
        yy = (y + j + side) % side

        def body(n, carry):
            at_rows = pl.ds(pl.multiple_of(n * strip, strip), strip)
            total = None if j == 0 else acc[part, at_rows, :]
            for xx in range(side):
                for c in range(2):
                    head = jnp.dot(obuf[o_slot(c, xx, yy), at_rows, :], wbuf[part, (yy * side + xx) * 2 + c], preferred_element_type=jnp.float32)
                    head = head.astype(jnp.bfloat16).astype(jnp.float32)
                    total = head if total is None else total + head
            acc[part, at_rows, :] = total
            return carry

        lax.fori_loop(0, line // strip, body, 0)

    def back_rows(device):
        return pl.ds(pl.multiple_of(device % (2 * side) * rows, rows), rows)

    for part in range(parts):
        project(part, 0)
        for j in (-1, 1, 2):
            for h in range(2):
                if (j, h) not in ((-1, 0), (1, 1)):
                    w_arrived(part, j, h)
            project(part, j)
        for k, dx in enumerate(steps):
            for dc in range(2):
                src = acc.at[part, back_rows(at(dx, 0, dc))]
                dst = rbuf.at[:, pl.ds(first_col(me, part), cols)]
                send(src, dst, back_send.at[part, k, dc], back_recv.at[part, k, dc], target(dx, 0, dc))
        if part == 0:
            w_relay(3)
    for part in range(parts):
        for k, dx in enumerate(steps):
            for dc in range(2):
                arrived(rbuf.at[:, pl.ds(first_col(at(-dx, 0, dc), part), cols)], back_recv.at[part, k, dc])

    def finish(at_cols):
        out_ref[:, at_cols] = res_ref[:, at_cols] + (rbuf[:, at_cols] + bias_ref[layer:layer + 1, at_cols])

    by_cols(width, finish)
    for copy in sent:
        copy.wait_send()


def attend_and_project(side, call_id, layer, qkv, ids, row_ids, weight, residual, bias):
    rows, width = residual.shape
    seq, dim = qkv.shape[0], weight.shape[2]
    groups = 2 * side * side
    parts = 4
    cols = width // (2 * side) // parts
    block = min(QUERY_BLOCK, rows * 2 * side)
    vmem = pl.BlockSpec(memory_space=pltpu.VMEM)
    dma = pltpu.SemaphoreType.DMA
    return pl.pallas_call(
        functools.partial(attend_kernel, side, layer),
        out_shape=jax.ShapeDtypeStruct((rows, width), jnp.float32),
        in_specs=[vmem, vmem, vmem, pl.BlockSpec(memory_space=pl.ANY), vmem, vmem],
        out_specs=vmem,
        scratch_shapes=[
            pltpu.VMEM((dim, width), jnp.bfloat16),
            pltpu.VMEM((parts, groups, dim, cols), jnp.bfloat16),
            pltpu.VMEM((groups, rows * 2 * side, dim), jnp.bfloat16),
            pltpu.VMEM((seq, dim), jnp.bfloat16),
            pltpu.VMEM((block, seq), jnp.float32),
            pltpu.VMEM((parts, rows * 2 * side, cols), jnp.float32),
            pltpu.VMEM((rows, width), jnp.float32),
            dma,
            dma((parts, side, 2)), dma((parts, side, 2)),
            dma((parts, 6)), dma((parts, 6)),
            dma((side,)), dma((side,)),
            dma((6,)), dma((6,)),
            dma((8,)), dma((8,)),
            dma((parts, side, 2)), dma((parts, side, 2)),
        ],
        compiler_params=pltpu.CompilerParams(collective_id=call_id, has_side_effects=True, vmem_limit_bytes=VMEM_LIMIT),
        name=f"attend_{call_id}",
    )(qkv, ids, row_ids, weight, residual, bias)


def solution(mesh):
    groups = mesh.shape["tp"]
    side = math.isqrt(groups // 2)
    assert 2 * side * side == groups and side == 4
    row_spec = P("dp", "tp", None)
    vec_spec = P()
    second = P(None, "tp")
    in_specs = (row_spec, P("dp", "tp"), vec_spec, vec_spec, P(None, None, None, "tp"), second, vec_spec, vec_spec, vec_spec, P(None, None, "tp"), second, second, vec_spec)

    def device_fn(tokens, doc_ids, norm1_gain, norm1_shift, qkv_weight, out_weight, out_bias, norm2_gain, norm2_shift, up_weight, up_bias, down_weight, down_bias):
        layers = norm1_gain.shape[0]
        id_cols = jnp.broadcast_to(doc_ids[0].astype(jnp.bfloat16)[:, None], (doc_ids.shape[1], 128))
        qkv_thirds = jnp.transpose(qkv_weight, (0, 2, 3, 1, 4))
        residual = tokens[0].astype(jnp.float32)
        for layer in range(layers):
            ids = [4 * layer + k for k in range(4)]
            tails = id_cols if layer == 0 else None
            qkv = gather_and_project(side, ids[0], layer, residual, norm1_gain, norm1_shift, qkv_thirds, norm1_gain, False, tails)
            if layer == 0:
                qkv, all_ids = qkv
                row_ids = all_ids[:, 0].astype(jnp.float32)[None]
            residual = attend_and_project(side, ids[1], layer, qkv, all_ids, row_ids, out_weight, residual, out_bias)
            hidden = gather_and_project(side, ids[2], layer, residual, norm2_gain, norm2_shift, up_weight, up_bias, True)
            residual = project_and_scatter(side, ids[3], layer, hidden, down_weight, residual, down_bias)
        return residual.astype(jnp.bfloat16)[None]

    return jax.shard_map(device_fn, mesh=mesh, in_specs=in_specs, out_specs=row_spec, check_vma=False)
```

profile of v0, /device:TPU:97, one launch (start us, length us, event | category | flops | bytes accessed | tf_op | source)
XLA Modules:
  0.0 576.8 jit_solution(13536686000208842186)
XLA Ops:
  0.0 0.7 convert_bitcast_fusion.1
  0.7 0.7 broadcast_in_dim.4.refs_0_
  1.3 2.1 bitcast_convert_fusion.res_ref
  3.4 63.9 %gather_0.1 = (bf16[2048,384]{1,0:T(8,128)(2,1)}, bf16[2048,128]{1,0:T(8,128)(2,1)}) custom-call(f32[64,4096]{1,0:T(8,128)} %bitcast_convert_fusion.res_ref, f32[2,4096]{1,0:T(2,128)} %b_ref.6, f32[2,4096]{1,0:T(2,128)} %shift_ref.6, bf16[2,3,1,4096,128]{4,3,2,1,0:T(8,128)(2,1)} %bitcast.9, f32[2,4096]{1,0:T(2,128)} %b_ref.6, ...), custom_call_target="tpu_custom_call" | custom-call | tf_op jit(solution)/shard_map/gather_0/pallas_call | solution.py:357
  67.4 1.9 convert_reduce_fusion
  69.2 65.8 %attend_1.1.res_ref = f32[64,4096]{1,0:T(8,128)} custom-call(bf16[2048,384]{1,0:T(8,128)(2,1)} %get-tuple-element.7.qkv_ref, bf16[2048,128]{1,0:T(8,128)(2,1)} %get-tuple-element.8.ids_ref, f32[1,2048]{1,0:T(1,128)} %bitcast.11, bf16[2,1,128,4096]{3,2,1,0:T(8,128)(2,1)} %w_hbm.9, f32[64,4096]{1,0:T(8,128)} %bitcast_convert_fusion.res_ref, f32[2,4096]{1,0:T(2,128)} %bias_ref.6), custom_call_target="tpu_custom_call" | custom-call | tf_op jit(solution)/shard_map/attend_1/pallas_call | solution.py:600
  135.1 59.2 %gather_2.1.act_ref = bf16[2048,512]{1,0:T(8,128)(2,1)} custom-call(f32[64,4096]{1,0:T(8,128)} %attend_1.1.res_ref, f32[2,4096]{1,0:T(2,128)} %gain_ref.7, f32[2,4096]{1,0:T(2,128)} %shift_ref.7, bf16[2,4096,512]{2,1,0:T(8,128)(2,1)} %w_hbm.10, f32[2,512]{1,0:T(2,128)} %b_ref.7), custom_call_target="tpu_custom_call" | custom-call | tf_op jit(solution)/shard_map/gather_2/pallas_call | solution.py:357
  194.3 98.4 %scatter_3.1.res_ref = f32[64,4096]{1,0:T(8,128)} custom-call(bf16[2048,512]{1,0:T(8,128)(2,1)} %gather_2.1.act_ref, bf16[2,512,4096]{2,1,0:T(8,128)(2,1)} %w_hbm.11, f32[64,4096]{1,0:T(8,128)} %attend_1.1.res_ref, f32[2,4096]{1,0:T(2,128)} %bias_ref.7), custom_call_target="tpu_custom_call" | custom-call | tf_op jit(solution)/shard_map/scatter_3/pallas_call | solution.py:195
  292.6 57.1 %gather_4.1.qkv_ref = bf16[2048,384]{1,0:T(8,128)(2,1)} custom-call(f32[64,4096]{1,0:T(8,128)} %scatter_3.1.res_ref, f32[2,4096]{1,0:T(2,128)} %b_ref.6, f32[2,4096]{1,0:T(2,128)} %shift_ref.6, bf16[2,3,1,4096,128]{4,3,2,1,0:T(8,128)(2,1)} %bitcast.10, f32[2,4096]{1,0:T(2,128)} %b_ref.6), custom_call_target="tpu_custom_call" | custom-call | tf_op jit(solution)/shard_map/gather_4/pallas_call | solution.py:357
  349.7 67.5 %attend_5.1.res_ref = f32[64,4096]{1,0:T(8,128)} custom-call(bf16[2048,384]{1,0:T(8,128)(2,1)} %gather_4.1.qkv_ref, bf16[2048,128]{1,0:T(8,128)(2,1)} %get-tuple-element.8.ids_ref, f32[1,2048]{1,0:T(1,128)} %bitcast.12, bf16[2,1,128,4096]{3,2,1,0:T(8,128)(2,1)} %w_hbm.9, f32[64,4096]{1,0:T(8,128)} %scatter_3.1.res_ref, f32[2,4096]{1,0:T(2,128)} %bias_ref.6), custom_call_target="tpu_custom_call" | custom-call | tf_op jit(solution)/shard_map/attend_5/pallas_call | solution.py:600
  417.2 59.2 %gather_6.1.act_ref = bf16[2048,512]{1,0:T(8,128)(2,1)} custom-call(f32[64,4096]{1,0:T(8,128)} %attend_5.1.res_ref, f32[2,4096]{1,0:T(2,128)} %gain_ref.7, f32[2,4096]{1,0:T(2,128)} %shift_ref.7, bf16[2,4096,512]{2,1,0:T(8,128)(2,1)} %w_hbm.10, f32[2,512]{1,0:T(2,128)} %b_ref.7), custom_call_target="tpu_custom_call" | custom-call | tf_op jit(solution)/shard_map/gather_6/pallas_call | solution.py:357
  476.4 97.8 %scatter_7.1 = f32[64,4096]{1,0:T(8,128)} custom-call(bf16[2048,512]{1,0:T(8,128)(2,1)} %gather_6.1.act_ref, bf16[2,512,4096]{2,1,0:T(8,128)(2,1)} %w_hbm.11, f32[64,4096]{1,0:T(8,128)} %attend_5.1.res_ref, f32[2,4096]{1,0:T(2,128)} %bias_ref.7), custom_call_target="tpu_custom_call" | custom-call | tf_op jit(solution)/shard_map/scatter_7/pallas_call | solution.py:195
  574.3 2.1 convert_bitcast_fusion
where the time goes:
time: 586 us; the launch traced here: 577 us
  Pallas kernels  569 us (97%)
  other arithmetic  6.66 us (1%)
    pallas_call x4, Pallas kernels, gather_and_project(): pl.pallas_call(functools.partial(gather_kernel, side, layer, gelu, tail),...  239 us
    pallas_call x2, Pallas kernels, project_and_scatter(): pl.pallas_call(functools.partial(scatter_kernel, side, layer), out_shape=...  196 us
    pallas_call x2, Pallas kernels, attend_and_project(): pl.pallas_call(functools.partial(attend_kernel, side, layer), out_shape=j...  133 us

commit v1 on v0

--- a/solution.py
+++ b/solution.py
@@ -247,104 +247,92 @@
         buf[place.me, :, pl.ds(width, tail)] = tails[...]
     place.barrier()
 
+    def pick(n, values):
+        value = values[0]
+        for k, other in enumerate(values):
+            value = jnp.where(n == k, other, value)
+        return value
+
     def view(i, j, h, core=None):
-        return buf.at[place.dev(i, j, core), pl.ds(h * half, half)]
+        return buf.at[place.dev(i, j, core), pl.ds(pl.multiple_of(h * half, half), half)]
 
     def wrap(k):
-        return (k + 1) % side - 1
+        return (k + side + 1) % side - 1
 
     def slot(i, j, h):
-        return ((i % side) * side + j % side) * 2 + h
-
-    sent = []
-
-    def send(i, j, h, axis, step):
-        there = (wrap(i - step), j) if axis == 0 else (i, wrap(j - step))
-        device = (place.first, place.second)[axis][step]
-        index = slot(i, j, h)
-        copy = pltpu.make_async_remote_copy(src_ref=view(i, j, h), dst_ref=view(i, j, h), send_sem=send_sem.at[axis * 2 + (step > 0), index], recv_sem=recv_sem.at[slot(*there, h)], device_id={"tp": device}, device_id_type=MESH)
-        copy.start()
-        sent.append(copy)
+        return ((i + side) % side * side + (j + side) % side) * 2 + h
+
+    def ring_copies(i, j, h):
+        own = (j == 0) & (i == 0)
+        begins = (h == 0, h == 1)
+        for axis, ahead in enumerate(((j == 0, i), (True, j))):
+            whole = own if axis == 0 else j == 0
+            for side_of, step in enumerate((1, -1)):
+                there = (wrap(i - step), j) if axis == 0 else (i, wrap(j - step))
+                device = (place.first, place.second)[axis][step]
+                condition = whole | (ahead[0] & (ahead[1] == -step) & begins[side_of])
+                yield condition, pltpu.make_async_remote_copy(src_ref=view(i, j, h), dst_ref=view(i, j, h), send_sem=send_sem.at[axis * 2 + side_of, slot(i, j, h)], recv_sem=recv_sem.at[slot(*there, h)], device_id={"tp": device}, device_id_type=MESH)
 
     def pair(i, j, h, core=None):
         index = slot(i, j, h)
         ref = view(i, j, h, core)
         return pltpu.make_async_remote_copy(src_ref=ref, dst_ref=ref, send_sem=pair_send.at[index], recv_sem=pair_recv.at[index], device_id={"tp": place.partner}, device_id_type=MESH)
 
-    def share(i, j, h):
-        copy = pair(i, j, h)
-        copy.start()
-        sent.append(copy)
-
     def arrived(i, j, h):
         ref = view(i, j, h)
         pltpu.make_async_remote_copy(src_ref=ref, dst_ref=ref, send_sem=send_sem.at[0, 0], recv_sem=recv_sem.at[slot(i, j, h)], device_id={"tp": place.me}, device_id_type=MESH).wait_recv()
 
-    def multiply(shards, core):
-        devs = [place.dev(i, j, core) for i, j in shards]
-        wide = w_ref.shape[1]
-        step = wide if wide % 256 else 256
+    def multiply(i, j):
+        devs = [place.dev(i, j), place.dev(i, j, 1 - place.core)]
         at = [pl.ds(pl.multiple_of(d * rows, rows), rows) for d in devs]
         if tail:
             for d, where in zip(devs, at):
                 tails_out[where, :] = buf[d, :, pl.ds(width, tail)]
-
-        def piece(cols):
-            lhs = jnp.concatenate([buf[d, :, pl.ds(0, width)] for d in devs], axis=0)
-            part = jnp.dot(lhs, w_ref[:, cols], preferred_element_type=jnp.float32)
-            if gelu:
-                part = jax.nn.gelu(part + b_ref[layer:layer + 1, cols], approximate=True)
-            part = part.astype(jnp.bfloat16)
-            for k, where in enumerate(at):
-                out[where, cols] = part[k * rows:(k + 1) * rows]
-
-        if step == wide:
-            piece(pl.ds(0, wide))
-        else:
-            def body(n, carry):
-                piece(pl.ds(pl.multiple_of(n * step, step), step))
-                return carry
-            lax.fori_loop(0, wide // step, body, 0)
-
-    def forward(i, j, h):
-        if j == 0:
-            if i == 0:
-                send(i, j, h, 0, 1)
-                send(i, j, h, 0, -1)
-            elif i == -1 and h == 0:
-                send(i, j, h, 0, 1)
-            elif i == 1 and h == 1:
-                send(i, j, h, 0, -1)
-            send(i, j, h, 1, 1)
-            send(i, j, h, 1, -1)
-        elif j == -1 and h == 0:
-            send(i, j, h, 1, 1)
-        elif j == 1 and h == 1:
-            send(i, j, h, 1, -1)
-        share(i, j, h)
-
-    for h in range(2):
-        forward(0, 0, h)
-    for load in loads:
-        load.wait()
-    cuts = (0, 4, 8, 12, 14, 16)
-    for start, stop in zip(cuts, cuts[1:]):
-        shards = GATHER_ORDER[start:stop]
-        lead = [(i, j, 1 if 1 in (i, j) and -1 not in (i, j) else 0) for i, j in shards if (i, j) != (0, 0)]
-        for i, j, h in lead + [(i, j, 1 - h) for i, j, h in lead]:
-            arrived(i, j, h)
-            forward(i, j, h)
-        for i, j in shards:
-            for h in range(2):
-                pair(i, j, h, 1 - place.core).wait_recv()
-
-        def both(k, carry):
-            multiply(shards, (place.core + k) % 2)
-            return carry
-
-        lax.fori_loop(0, 2, both, 0)
-    for copy in sent:
-        copy.wait_send()
+        lhs = jnp.concatenate([buf[d, :, pl.ds(0, width)] for d in devs], axis=0)
+        part = jnp.dot(lhs, w_ref[...], preferred_element_type=jnp.float32)
+        if gelu:
+            part = jax.nn.gelu(part + b_ref[layer:layer + 1, :], approximate=True)
+        part = part.astype(jnp.bfloat16)
+        for k, where in enumerate(at):
+            out[where, :] = part[k * rows:(k + 1) * rows]
+
+    firsts = [at[0] for at in GATHER_ORDER]
+    seconds = [at[1] for at in GATHER_ORDER]
+    leads = [int(1 in at and -1 not in at) for at in GATHER_ORDER]
+
+    def take(n, carry):
+        i, j, lead = pick(n, firsts), pick(n, seconds), pick(n, leads)
+        for k in range(2):
+            h = (lead + k) % 2
+
+            @pl.when(n > 0)
+            def _():
+                arrived(i, j, h)
+
+            for condition, copy in ring_copies(i, j, h):
+                pl.when(condition)(copy.start)
+            pair(i, j, h).start()
+
+        @pl.when(n == 0)
+        def _():
+            for load in loads:
+                load.wait()
+
+        for h in range(2):
+            pair(i, j, h, 1 - place.core).wait_recv()
+        multiply(i, j)
+        return carry
+
+    def drain(n, carry):
+        i, j = pick(n, firsts), pick(n, seconds)
+        for h in range(2):
+            for condition, copy in ring_copies(i, j, h):
+                pl.when(condition)(copy.wait_send)
+            pair(i, j, h).wait_send()
+        return carry
+
+    lax.fori_loop(0, len(GATHER_ORDER), take, 0)
+    lax.fori_loop(0, len(GATHER_ORDER), drain, 0)
 
 
 def gather_and_project(side, call_id, layer, residual, gain, shift, weight, bias, gelu, tails=None):
@@ -542,17 +530,21 @@
 
     strip = min(block, line)
 
-    def project(part, j):
+    def heads_of(part, at_rows, j, total):
         yy = (y + j + side) % side
-
+        for xx in range(side):
+            for c in range(2):
+                head = jnp.dot(obuf[o_slot(c, xx, yy), at_rows, :], wbuf[part, (yy * side + xx) * 2 + c], preferred_element_type=jnp.float32)
+                total = total + head.astype(jnp.bfloat16).astype(jnp.float32)
+        return total
+
+    def project(part, last):
         def body(n, carry):
             at_rows = pl.ds(pl.multiple_of(n * strip, strip), strip)
-            total = None if j == 0 else acc[part, at_rows, :]
-            for xx in range(side):
-                for c in range(2):
-                    head = jnp.dot(obuf[o_slot(c, xx, yy), at_rows, :], wbuf[part, (yy * side + xx) * 2 + c], preferred_element_type=jnp.float32)
-                    head = head.astype(jnp.bfloat16).astype(jnp.float32)
-                    total = head if total is None else total + head
+            if last:
+                total = heads_of(part, at_rows, 2, acc[part, at_rows, :])
+            else:
+                total = lax.fori_loop(0, 3, lambda k, t: heads_of(part, at_rows, (k + 1) % 3 - 1, t), jnp.zeros((strip, cols), jnp.float32))
             acc[part, at_rows, :] = total
             return carry
 
@@ -562,12 +554,12 @@
         return pl.ds(pl.multiple_of(device % (2 * side) * rows, rows), rows)
 
     for part in range(parts):
-        project(part, 0)
-        for j in (-1, 1, 2):
-            for h in range(2):
-                if (j, h) not in ((-1, 0), (1, 1)):
-                    w_arrived(part, j, h)
-            project(part, j)
+        w_arrived(part, -1, 1)
+        w_arrived(part, 1, 0)
+        project(part, False)
+        for h in range(2):
+            w_arrived(part, 2, h)
+        project(part, True)
         for k, dx in enumerate(steps):
             for dc in range(2):
                 src = acc.at[part, back_rows(at(dx, 0, dc))]

time: 586 us -> 578 us (0.986); the launches traced: 577 us -> 577 us
  no operation moved by 1% of the time
where the time goes in v1:
time: 578 us; the launch traced here: 577 us
  Pallas kernels  570 us (99%)
  other arithmetic  6.66 us (1%)
    pallas_call x4, Pallas kernels, gather_and_project(): pl.pallas_call(functools.partial(gather_kernel, side, layer, gelu, tail),...  243 us
    pallas_call x2, Pallas kernels, project_and_scatter(): pl.pallas_call(functools.partial(scatter_kernel, side, layer), out_shape=...  197 us
    pallas_call x2, Pallas kernels, attend_and_project(): pl.pallas_call(functools.partial(attend_kernel, side, layer), out_shape=j...  130 us

profile of v1, /device:TPU:97, one launch (start us, length us, event | category | flops | bytes accessed | tf_op | source)
XLA Modules:
  0.0 577.4 jit_solution(15319310727357600973)
XLA Ops:
  0.0 0.7 convert_bitcast_fusion.1
  0.7 0.7 broadcast_in_dim.4.refs_0_
  1.3 2.1 bitcast_convert_fusion.res_ref
  3.4 64.8 %gather_0.1 = (bf16[2048,384]{1,0:T(8,128)(2,1)}, bf16[2048,128]{1,0:T(8,128)(2,1)}) custom-call(f32[64,4096]{1,0:T(8,128)} %bitcast_convert_fusion.res_ref, f32[2,4096]{1,0:T(2,128)} %b_ref.6, f32[2,4096]{1,0:T(2,128)} %shift_ref.6, bf16[2,3,1,4096,128]{4,3,2,1,0:T(8,128)(2,1)} %bitcast.9, f32[2,4096]{1,0:T(2,128)} %b_ref.6, ...), custom_call_target="tpu_custom_call" | custom-call | tf_op jit(solution)/shard_map/gather_0/pallas_call | solution.py:345
  68.2 1.9 convert_reduce_fusion
  70.1 64.8 %attend_1.1.res_ref = f32[64,4096]{1,0:T(8,128)} custom-call(bf16[2048,384]{1,0:T(8,128)(2,1)} %get-tuple-element.7.qkv_ref, bf16[2048,128]{1,0:T(8,128)(2,1)} %get-tuple-element.8.ids_ref, f32[1,2048]{1,0:T(1,128)} %bitcast.11, bf16[2,1,128,4096]{3,2,1,0:T(8,128)(2,1)} %w_hbm.9, f32[64,4096]{1,0:T(8,128)} %bitcast_convert_fusion.res_ref, f32[2,4096]{1,0:T(2,128)} %bias_ref.6), custom_call_target="tpu_custom_call" | custom-call | tf_op jit(solution)/shard_map/attend_1/pallas_call | solution.py:592
  134.9 59.9 %gather_2.1.act_ref = bf16[2048,512]{1,0:T(8,128)(2,1)} custom-call(f32[64,4096]{1,0:T(8,128)} %attend_1.1.res_ref, f32[2,4096]{1,0:T(2,128)} %gain_ref.7, f32[2,4096]{1,0:T(2,128)} %shift_ref.7, bf16[2,4096,512]{2,1,0:T(8,128)(2,1)} %w_hbm.10, f32[2,512]{1,0:T(2,128)} %b_ref.7), custom_call_target="tpu_custom_call" | custom-call | tf_op jit(solution)/shard_map/gather_2/pallas_call | solution.py:345
  194.8 98.6 %scatter_3.1.res_ref = f32[64,4096]{1,0:T(8,128)} custom-call(bf16[2048,512]{1,0:T(8,128)(2,1)} %gather_2.1.act_ref, bf16[2,512,4096]{2,1,0:T(8,128)(2,1)} %w_hbm.11, f32[64,4096]{1,0:T(8,128)} %attend_1.1.res_ref, f32[2,4096]{1,0:T(2,128)} %bias_ref.7), custom_call_target="tpu_custom_call" | custom-call | tf_op jit(solution)/shard_map/scatter_3/pallas_call | solution.py:195
  293.4 58.3 %gather_4.1.qkv_ref = bf16[2048,384]{1,0:T(8,128)(2,1)} custom-call(f32[64,4096]{1,0:T(8,128)} %scatter_3.1.res_ref, f32[2,4096]{1,0:T(2,128)} %b_ref.6, f32[2,4096]{1,0:T(2,128)} %shift_ref.6, bf16[2,3,1,4096,128]{4,3,2,1,0:T(8,128)(2,1)} %bitcast.10, f32[2,4096]{1,0:T(2,128)} %b_ref.6), custom_call_target="tpu_custom_call" | custom-call | tf_op jit(solution)/shard_map/gather_4/pallas_call | solution.py:345
  351.8 65.3 %attend_5.1.res_ref = f32[64,4096]{1,0:T(8,128)} custom-call(bf16[2048,384]{1,0:T(8,128)(2,1)} %gather_4.1.qkv_ref, bf16[2048,128]{1,0:T(8,128)(2,1)} %get-tuple-element.8.ids_ref, f32[1,2048]{1,0:T(1,128)} %bitcast.12, bf16[2,1,128,4096]{3,2,1,0:T(8,128)(2,1)} %w_hbm.9, f32[64,4096]{1,0:T(8,128)} %scatter_3.1.res_ref, f32[2,4096]{1,0:T(2,128)} %bias_ref.6), custom_call_target="tpu_custom_call" | custom-call | tf_op jit(solution)/shard_map/attend_5/pallas_call | solution.py:592
  417.0 59.8 %gather_6.1.act_ref = bf16[2048,512]{1,0:T(8,128)(2,1)} custom-call(f32[64,4096]{1,0:T(8,128)} %attend_5.1.res_ref, f32[2,4096]{1,0:T(2,128)} %gain_ref.7, f32[2,4096]{1,0:T(2,128)} %shift_ref.7, bf16[2,4096,512]{2,1,0:T(8,128)(2,1)} %w_hbm.10, f32[2,512]{1,0:T(2,128)} %b_ref.7), custom_call_target="tpu_custom_call" | custom-call | tf_op jit(solution)/shard_map/gather_6/pallas_call | solution.py:345
  476.8 98.6 %scatter_7.1 = f32[64,4096]{1,0:T(8,128)} custom-call(bf16[2048,512]{1,0:T(8,128)(2,1)} %gather_6.1.act_ref, bf16[2,512,4096]{2,1,0:T(8,128)(2,1)} %w_hbm.11, f32[64,4096]{1,0:T(8,128)} %attend_5.1.res_ref, f32[2,4096]{1,0:T(2,128)} %bias_ref.7), custom_call_target="tpu_custom_call" | custom-call | tf_op jit(solution)/shard_map/scatter_7/pallas_call | solution.py:195
  575.4 2.1 convert_bitcast_fusion

commit v2 on v1

--- a/solution.py
+++ b/solution.py
@@ -34,12 +34,17 @@
         dy = j * (1 - core) + i * core
         return (((self.y + dy + self.side) % self.side) * self.side + (self.x + dx + self.side) % self.side) * 2 + core
 
-    def barrier(self):
-        sem = pltpu.get_barrier_semaphore()
-        others = [self.first[1], self.first[-1], self.second[1], self.second[-1], self.partner]
-        for other in others:
-            pl.semaphore_signal(sem, inc=1, device_id={"tp": other}, device_id_type=MESH)
-        pl.semaphore_wait(sem, len(others))
+    def neighbours(self):
+        return [self.first[1], self.first[-1], self.second[1], self.second[-1], self.partner]
+
+
+def announce(others):
+    for other in others:
+        pl.semaphore_signal(pltpu.get_barrier_semaphore(), inc=1, device_id={"tp": other}, device_id_type=MESH)
+
+
+def meet(others):
+    pl.semaphore_wait(pltpu.get_barrier_semaphore(), len(others))
 
 
 def by_cols(width, fn):
@@ -58,7 +63,7 @@
     place = Place(side)
     rows, width = res_ref.shape
     half = rows // 2
-    place.barrier()
+    announce(place.neighbours())
     load_w.wait()
 
     def remote(src, dst, slot, device):
@@ -98,6 +103,8 @@
             if g >= 2:
                 pair_copy(g - 2, jj).wait_send()
         product(1 - place.core, g, snd.at[g % 2])
+        if g == 0:
+            meet(place.neighbours())
         for jj in range(side):
             pair_copy(g, jj).start()
         product(place.core, g, own.at[g])
@@ -222,30 +229,22 @@
 GATHER_ORDER = sorted(((i, j) for i in STEPS for j in STEPS), key=lambda at: (2 * abs(at[0]) + 3 * abs(at[1]), at))
 
 
-def gather_kernel(side, layer, gelu, tail, res_ref, gain_ref, shift_ref, w_hbm, b_ref, *refs):
-    tails, refs = (refs[0], refs[1:]) if tail else (None, refs)
-    out, refs = refs[0], refs[1:]
-    tails_out, refs = (refs[0], refs[1:]) if tail else (None, refs)
-    (w_ref, buf, w_sem, send_sem, recv_sem, pair_send, pair_recv) = refs
-    if len(w_hbm.shape) == 3:
-        loads = [pltpu.make_async_copy(w_hbm.at[layer], w_ref, w_sem.at[0])]
-    else:
-        each = w_hbm.shape[4]
-        loads = [pltpu.make_async_copy(w_hbm.at[layer, k, 0], w_ref.at[:, pl.ds(k * each, each)], w_sem.at[k]) for k in range(w_hbm.shape[1])]
-    for load in loads:
-        load.start()
-    place = Place(side)
+def gather_body(place, layer, gelu, res_ref, gain_ref, shift_ref, w_ref, loads, b_ref, out, buf, sems, tails=None, tails_out=None, ready=None, hook=None):
+    send_sem, recv_sem, pair_send, pair_recv = sems
+    side = place.side
     rows, width = res_ref.shape
+    tail = 0 if tails is None else tails.shape[1]
     half = rows // 2
     for at in (pl.ds(0, half), pl.ds(half, half)):
-        residual = res_ref[at, :]
+        residual = res_ref[at, :].astype(jnp.float32)
         centered = residual - jnp.mean(residual, axis=-1, keepdims=True)
         variance = jnp.mean(centered * centered, axis=-1, keepdims=True)
         normed = centered * lax.rsqrt(variance + 1e-5) * gain_ref[layer:layer + 1, :] + shift_ref[layer:layer + 1, :]
         buf[place.me, at, pl.ds(0, width)] = normed.astype(jnp.bfloat16)
     if tail:
         buf[place.me, :, pl.ds(width, tail)] = tails[...]
-    place.barrier()
+    if ready is not None:
+        ready()
 
     def pick(n, values):
         value = values[0]
@@ -331,48 +330,22 @@
             pair(i, j, h).wait_send()
         return carry
 
-    lax.fori_loop(0, len(GATHER_ORDER), take, 0)
-    lax.fori_loop(0, len(GATHER_ORDER), drain, 0)
-
-
-def gather_and_project(side, call_id, layer, residual, gain, shift, weight, bias, gelu, tails=None):
-    rows, width = residual.shape
-    tail = 0 if tails is None else tails.shape[1]
-    extra = [] if tails is None else [tails]
-    groups = 2 * side * side
-    wide = weight.shape[2] if weight.ndim == 3 else weight.shape[1] * weight.shape[4]
-    vmem = pl.BlockSpec(memory_space=pltpu.VMEM)
-    outs = pl.pallas_call(
-        functools.partial(gather_kernel, side, layer, gelu, tail),
-        out_shape=[jax.ShapeDtypeStruct((groups * rows, wide), jnp.bfloat16)] + [jax.ShapeDtypeStruct((groups * rows, tail), jnp.bfloat16) for _ in extra],
-        in_specs=[vmem, vmem, vmem, pl.BlockSpec(memory_space=pl.ANY), vmem] + [vmem for _ in extra],
-        out_specs=[vmem] * (1 + len(extra)),
-        scratch_shapes=[
-            pltpu.VMEM((width, wide), jnp.bfloat16),
-            pltpu.VMEM((groups, rows, width + tail), jnp.bfloat16),
-            pltpu.SemaphoreType.DMA((3,)),
-            pltpu.SemaphoreType.DMA((4, groups)),
-            pltpu.SemaphoreType.DMA((groups,)),
-            pltpu.SemaphoreType.DMA((groups,)),
-            pltpu.SemaphoreType.DMA((groups,)),
-        ],
-        compiler_params=pltpu.CompilerParams(collective_id=call_id, has_side_effects=True, vmem_limit_bytes=VMEM_LIMIT),
-        name=f"gather_{call_id}",
-    )(residual, gain, shift, weight, bias, *extra)
-    return outs if len(outs) > 1 else outs[0]
+    last = max(n for n, at in enumerate(GATHER_ORDER) if at[1] != 2) + 1
+    lax.fori_loop(0, last, take, 0)
+    if hook is not None:
+        hook()
+    lax.fori_loop(last, len(GATHER_ORDER), take, 0)
+    return lambda: lax.fori_loop(0, len(GATHER_ORDER), drain, 0)
 
 
 QUERY_BLOCK = 256
 RING = ((-1, 0), (1, 1), (-1, 1), (1, 0), (2, 0), (2, 1))
 
 
-def attend_kernel(side, layer, qkv_ref, ids_ref, row_ids_ref, w_hbm, res_ref, bias_ref, out_ref, w_own, wbuf, obuf, o_own, scores, acc, rbuf, load_sem, ws_send, ws_recv, wg_send, wg_recv, os_send, os_recv, og_send, og_recv, op_send, op_recv, back_send, back_recv):
-    load_w = pltpu.make_async_copy(w_hbm.at[layer, 0], w_own, load_sem)
-    load_w.start()
-    me = lax.axis_index("tp")
-    core = me % 2
-    x = me // 2 % side
-    y = me // 2 // side
+def attend_body(place, layer, qkv_ref, ids_ref, row_ids_ref, load_w, res_ref, bias_ref, out_ref, bufs, sems):
+    w_own, wbuf, obuf, o_own, scores, acc, rbuf = bufs
+    ws_send, ws_recv, wg_send, wg_recv, os_send, os_recv, og_send, og_recv, op_send, op_recv, back_send, back_recv = sems
+    side, me, core, x, y = place.side, place.me, place.core, place.x, place.y
     rows, width = res_ref.shape
     dim = w_own.shape[0]
     share = width // (2 * side)
@@ -385,12 +358,6 @@
 
     peers = [at(dx, 0, dc) for dx in steps for dc in (1, 0) if (dx, dc) != (0, 0)]
     columns = [at(0, dy, 0) for dy in steps[:3]]
-    barrier = pltpu.get_barrier_semaphore()
-    for peer in peers + columns:
-        pl.semaphore_signal(barrier, inc=1, device_id={"tp": peer}, device_id_type=MESH)
-    pl.semaphore_wait(barrier, len(peers) + len(columns))
-    load_w.wait()
-
     sent = []
 
     def send(src, dst, send_sem, recv_sem, device):
@@ -410,11 +377,13 @@
     def first_col(device, part):
         return pl.multiple_of(device % (2 * side) * share + part * cols, 128)
 
-    for part in range(parts):
-        for k, dx in enumerate(steps):
-            for dc in range(2):
-                src = w_own.at[:, pl.ds(first_col(at(dx, 0, dc), part), cols)]
-                send(src, wbuf.at[part, me], ws_send.at[part, k, dc], ws_recv.at[part, k, dc], target(dx, 0, dc))
+    def begin():
+        load_w.wait()
+        for part in range(parts):
+            for k, dx in enumerate(steps):
+                for dc in range(2):
+                    src = w_own.at[:, pl.ds(first_col(at(dx, 0, dc), part), cols)]
+                    send(src, wbuf.at[part, me], ws_send.at[part, k, dc], ws_recv.at[part, k, dc], target(dx, 0, dc))
 
     def w_slots(part, j, h):
         return wbuf.at[part, pl.ds(((y + j + side) % side) * 2 * side + h * side, side)]
@@ -498,35 +467,6 @@
 
     def o_share(k, i, h):
         send(o_slots(i, h), o_slots(i, h), op_send.at[k], op_recv.at[k], at(0, 0, 1))
-
-    attend_line(0)
-    attend_line(1)
-    w_first(0)
-    attend_line(2)
-    w_first(1)
-    attend_line(3)
-    w_relay(0)
-    for k, dy in enumerate(steps):
-        arrived(obuf.at[o_slot(core, x, (y - dy + side) % side)], os_recv.at[k])
-    for h in range(2):
-        o_send(0, h, 1, RING.index((-1, h)))
-        o_send(0, 1 - h, -1, RING.index((1, 1 - h)))
-    w_first(2)
-    for h in range(2):
-        o_share(h, 0, h)
-    w_relay(1)
-    w_first(3)
-    for k, (i, h) in enumerate(RING):
-        arrived(o_slots(i, h), og_recv.at[k])
-        if (i, h) == (-1, 0):
-            o_send(i, h, 1, RING.index((2, 0)))
-        if (i, h) == (1, 1):
-            o_send(i, h, -1, RING.index((2, 1)))
-        o_share(2 + k, i, h)
-        if k == 3:
-            w_relay(2)
-    for k, (i, h) in enumerate(((0, 0), (0, 1)) + RING):
-        arrived(o_slots(i, h, 1), op_recv.at[k])
 
     strip = min(block, line)
 
@@ -553,56 +493,138 @@
     def back_rows(device):
         return pl.ds(pl.multiple_of(device % (2 * side) * rows, rows), rows)
 
-    for part in range(parts):
-        w_arrived(part, -1, 1)
-        w_arrived(part, 1, 0)
-        project(part, False)
+    def finish(at_cols):
+        out_ref[:, at_cols] = res_ref[:, at_cols].astype(jnp.float32) + (rbuf[:, at_cols] + bias_ref[layer:layer + 1, at_cols])
+
+    def proceed():
+        attend_line(0)
+        attend_line(1)
+        w_first(0)
+        attend_line(2)
+        w_first(1)
+        attend_line(3)
+        w_relay(0)
+        for k, dy in enumerate(steps):
+            arrived(obuf.at[o_slot(core, x, (y - dy + side) % side)], os_recv.at[k])
         for h in range(2):
-            w_arrived(part, 2, h)
-        project(part, True)
-        for k, dx in enumerate(steps):
-            for dc in range(2):
-                src = acc.at[part, back_rows(at(dx, 0, dc))]
-                dst = rbuf.at[:, pl.ds(first_col(me, part), cols)]
-                send(src, dst, back_send.at[part, k, dc], back_recv.at[part, k, dc], target(dx, 0, dc))
-        if part == 0:
-            w_relay(3)
-    for part in range(parts):
-        for k, dx in enumerate(steps):
-            for dc in range(2):
-                arrived(rbuf.at[:, pl.ds(first_col(at(-dx, 0, dc), part), cols)], back_recv.at[part, k, dc])
-
-    def finish(at_cols):
-        out_ref[:, at_cols] = res_ref[:, at_cols] + (rbuf[:, at_cols] + bias_ref[layer:layer + 1, at_cols])
-
-    by_cols(width, finish)
-    for copy in sent:
-        copy.wait_send()
-
-
-def attend_and_project(side, call_id, layer, qkv, ids, row_ids, weight, residual, bias):
+            o_send(0, h, 1, RING.index((-1, h)))
+            o_send(0, 1 - h, -1, RING.index((1, 1 - h)))
+        w_first(2)
+        for h in range(2):
+            o_share(h, 0, h)
+        w_relay(1)
+        w_first(3)
+        for k, (i, h) in enumerate(RING):
+            arrived(o_slots(i, h), og_recv.at[k])
+            if (i, h) == (-1, 0):
+                o_send(i, h, 1, RING.index((2, 0)))
+            if (i, h) == (1, 1):
+                o_send(i, h, -1, RING.index((2, 1)))
+            o_share(2 + k, i, h)
+            if k == 3:
+                w_relay(2)
+        for k, (i, h) in enumerate(((0, 0), (0, 1)) + RING):
+            arrived(o_slots(i, h, 1), op_recv.at[k])
+
+        for part in range(parts):
+            w_arrived(part, -1, 1)
+            w_arrived(part, 1, 0)
+            project(part, False)
+            for h in range(2):
+                w_arrived(part, 2, h)
+            project(part, True)
+            for k, dx in enumerate(steps):
+                for dc in range(2):
+                    src = acc.at[part, back_rows(at(dx, 0, dc))]
+                    dst = rbuf.at[:, pl.ds(first_col(me, part), cols)]
+                    send(src, dst, back_send.at[part, k, dc], back_recv.at[part, k, dc], target(dx, 0, dc))
+            if part == 0:
+                w_relay(3)
+        for part in range(parts):
+            for k, dx in enumerate(steps):
+                for dc in range(2):
+                    arrived(rbuf.at[:, pl.ds(first_col(at(-dx, 0, dc), part), cols)], back_recv.at[part, k, dc])
+        by_cols(width, finish)
+
+    def drain():
+        for copy in sent:
+            copy.wait_send()
+
+    return peers + columns, begin, proceed, drain
+
+
+def front_kernel(side, layer, first, res_ref, ids_in, row_ids_in, gain1_ref, shift1_ref, w_qkv, w_out, bias_ref, gain2_ref, shift2_ref, w_up, b_ref, *refs):
+    out_ref, hidden_ref, refs = refs[0], refs[1], refs[2:]
+    ids_ref, row_ids_ref = ids_in, row_ids_in
+    if first:
+        ids_ref, row_ids_ref, refs = refs[0], refs[1], refs[2:]
+    w_qkv_ref, w_up_ref, qkv_ref, buf1, buf2, refs = *refs[:5], refs[5:]
+    bufs, w_sem, refs = refs[:7], refs[7], refs[8:]
+    sems1, sems2, sems = refs[:4], refs[4:8], refs[8:]
+    thirds = w_qkv.shape[1]
+    each = w_qkv.shape[4]
+    loads = [pltpu.make_async_copy(w_qkv.at[layer, k, 0], w_qkv_ref.at[:, pl.ds(k * each, each)], w_sem.at[k]) for k in range(thirds)]
+    load_out = pltpu.make_async_copy(w_out.at[layer, 0], bufs[0], w_sem.at[thirds])
+    load_up = pltpu.make_async_copy(w_up.at[layer], w_up_ref, w_sem.at[thirds + 1])
+    for load in loads + [load_out, load_up]:
+        load.start()
+    place = Place(side)
+    others, begin, proceed, drain = attend_body(place, layer, qkv_ref, ids_ref, row_ids_ref, load_out, res_ref, bias_ref, out_ref, bufs, sems)
+    announce(others)
+    drain1 = gather_body(place, layer, False, res_ref, gain1_ref, shift1_ref, w_qkv_ref, loads, None, qkv_ref, buf1, sems1, ids_in if first else None, ids_ref if first else None, lambda: meet(others), begin)
+    if first:
+        step = ids_ref.shape[1]
+
+        def turn(n, carry):
+            at = pl.ds(pl.multiple_of(n * step, step), step)
+            row_ids_ref[:, at] = jnp.transpose(ids_ref[at, :].astype(jnp.float32))[0:1]
+            return carry
+
+        lax.fori_loop(0, ids_ref.shape[0] // step, turn, 0)
+    proceed()
+    drain2 = gather_body(place, layer, True, out_ref, gain2_ref, shift2_ref, w_up_ref, [load_up], b_ref, hidden_ref, buf2, sems2)
+    drain1()
+    drain()
+    drain2()
+
+
+def front(side, call_id, layer, first, residual, ids, row_ids, gain1, shift1, w_qkv, w_out, out_bias, gain2, shift2, w_up, up_bias):
     rows, width = residual.shape
-    seq, dim = qkv.shape[0], weight.shape[2]
+    dim = w_out.shape[2]
     groups = 2 * side * side
+    seq = groups * rows
+    line = rows * 2 * side
     parts = 4
     cols = width // (2 * side) // parts
-    block = min(QUERY_BLOCK, rows * 2 * side)
+    block = min(QUERY_BLOCK, line)
+    tail = ids.shape[1]
     vmem = pl.BlockSpec(memory_space=pltpu.VMEM)
+    hbm = pl.BlockSpec(memory_space=pl.ANY)
     dma = pltpu.SemaphoreType.DMA
+    gather_sems = [dma((4, groups)), dma((groups,)), dma((groups,)), dma((groups,))]
+    shapes = [((rows, width), jnp.float32), ((seq, w_up.shape[2]), jnp.bfloat16)]
+    if first:
+        shapes += [((seq, tail), jnp.bfloat16), ((1, seq), jnp.float32)]
     return pl.pallas_call(
-        functools.partial(attend_kernel, side, layer),
-        out_shape=jax.ShapeDtypeStruct((rows, width), jnp.float32),
-        in_specs=[vmem, vmem, vmem, pl.BlockSpec(memory_space=pl.ANY), vmem, vmem],
-        out_specs=vmem,
+        functools.partial(front_kernel, side, layer, first),
+        out_shape=[jax.ShapeDtypeStruct(*shape) for shape in shapes],
+        in_specs=[vmem] * 5 + [hbm, hbm] + [vmem] * 3 + [hbm, vmem],
+        out_specs=[vmem] * len(shapes),
         scratch_shapes=[
+            pltpu.VMEM((width, w_qkv.shape[1] * dim), jnp.bfloat16),
+            pltpu.VMEM((width, w_up.shape[2]), jnp.bfloat16),
+            pltpu.VMEM((seq, w_qkv.shape[1] * dim), jnp.bfloat16),
+            pltpu.VMEM((groups, rows, width + (tail if first else 0)), jnp.bfloat16),
+            pltpu.VMEM((groups, rows, width), jnp.bfloat16),
             pltpu.VMEM((dim, width), jnp.bfloat16),
             pltpu.VMEM((parts, groups, dim, cols), jnp.bfloat16),
-            pltpu.VMEM((groups, rows * 2 * side, dim), jnp.bfloat16),
+            pltpu.VMEM((groups, line, dim), jnp.bfloat16),
             pltpu.VMEM((seq, dim), jnp.bfloat16),
             pltpu.VMEM((block, seq), jnp.float32),
-            pltpu.VMEM((parts, rows * 2 * side, cols), jnp.float32),
+            pltpu.VMEM((parts, line, cols), jnp.float32),
             pltpu.VMEM((rows, width), jnp.float32),
-            dma,
+            dma((w_qkv.shape[1] + 2,)),
+            *gather_sems, *gather_sems,
             dma((parts, side, 2)), dma((parts, side, 2)),
             dma((parts, 6)), dma((parts, 6)),
             dma((side,)), dma((side,)),
@@ -611,8 +633,8 @@
             dma((parts, side, 2)), dma((parts, side, 2)),
         ],
         compiler_params=pltpu.CompilerParams(collective_id=call_id, has_side_effects=True, vmem_limit_bytes=VMEM_LIMIT),
-        name=f"attend_{call_id}",
-    )(qkv, ids, row_ids, weight, residual, bias)
+        name=f"front_{call_id}",
+    )(residual, ids, row_ids, gain1, shift1, w_qkv, w_out, out_bias, gain2, shift2, w_up, up_bias)
 
 
 def solution(mesh):
@@ -628,17 +650,14 @@
         layers = norm1_gain.shape[0]
         id_cols = jnp.broadcast_to(doc_ids[0].astype(jnp.bfloat16)[:, None], (doc_ids.shape[1], 128))
         qkv_thirds = jnp.transpose(qkv_weight, (0, 2, 3, 1, 4))
-        residual = tokens[0].astype(jnp.float32)
+        residual = tokens[0]
+        all_ids, row_ids = id_cols, jnp.zeros((1, 128), jnp.float32)
         for layer in range(layers):
-            ids = [4 * layer + k for k in range(4)]
-            tails = id_cols if layer == 0 else None
-            qkv = gather_and_project(side, ids[0], layer, residual, norm1_gain, norm1_shift, qkv_thirds, norm1_gain, False, tails)
-            if layer == 0:
-                qkv, all_ids = qkv
-                row_ids = all_ids[:, 0].astype(jnp.float32)[None]
-            residual = attend_and_project(side, ids[1], layer, qkv, all_ids, row_ids, out_weight, residual, out_bias)
-            hidden = gather_and_project(side, ids[2], layer, residual, norm2_gain, norm2_shift, up_weight, up_bias, True)
-            residual = project_and_scatter(side, ids[3], layer, hidden, down_weight, residual, down_bias)
+            first = layer == 0
+            residual, hidden, *made = front(side, 2 * layer, layer, first, residual, all_ids, row_ids, norm1_gain, norm1_shift, qkv_thirds, out_weight, out_bias, norm2_gain, norm2_shift, up_weight, up_bias)
+            if first:
+                all_ids, row_ids = made
+            residual = project_and_scatter(side, 2 * layer + 1, layer, hidden, down_weight, residual, down_bias)
         return residual.astype(jnp.bfloat16)[None]
 
     return jax.shard_map(device_fn, mesh=mesh, in_specs=in_specs, out_specs=row_spec, check_vma=False)

time: 578 us -> 561 us (0.971)
  Pallas kernels: 570 us -> 557 us
    pallas_call x6 -> x2, Pallas kernels: 373 us -> 359 us  [front(): pl.pallas_call(functools.partial(front_kernel, side, layer, first), out_s...]
where the time goes in v2:
time: 561 us
  Pallas kernels  557 us (99%)
    pallas_call x2, Pallas kernels, front(): pl.pallas_call(functools.partial(front_kernel, side, layer, first), out_s...  359 us
    pallas_call x2, Pallas kernels, project_and_scatter(): pl.pallas_call(functools.partial(scatter_kernel, side, layer), out_shape=...  197 us

profile of v2, /device:TPU:97, one launch (start us, length us, event | category | flops | bytes accessed | tf_op | source)
XLA Modules:
  0.0 560.9 jit_solution(10952277037448586532)
XLA Ops:
  0.0 0.7 convert_bitcast_fusion.1
  0.7 0.7 broadcast_in_dim.12.ids_in
  1.3 0.5 broadcast_in_dim.13.row_ids_in
  1.9 183.1 %front_0.1 = (f32[64,4096]{1,0:T(8,128)}, bf16[2048,512]{1,0:T(8,128)(2,1)}, bf16[2048,128]{1,0:T(8,128)(2,1)}, f32[1,2048]{1,0:T(1,128)}) custom-call(bf16[64,4096]{1,0:T(8,128)(2,1)} %bitcast.8, bf16[64,128]{1,0:T(8,128)(2,1)} %broadcast_in_dim.12.ids_in, f32[1,128]{1,0:T(1,128)} %broadcast_in_dim.13.row_ids_in, f32[2,4096]{1,0:T(2,128)} %gain1_ref.3, ...), custom_call_target="tpu_custom_call" | custom-call | tf_op jit(solution)/shard_map/front_0/pallas_call | solution.py:608
  185.0 98.6 %scatter_1.1.res_ref = f32[64,4096]{1,0:T(8,128)} custom-call(bf16[2048,512]{1,0:T(8,128)(2,1)} %get-tuple-element.11.act_ref, bf16[2,512,4096]{2,1,0:T(8,128)(2,1)} %w_hbm.3, f32[64,4096]{1,0:T(8,128)} %get-tuple-element.12.res_ref, f32[2,4096]{1,0:T(2,128)} %bias_ref.7), custom_call_target="tpu_custom_call" | custom-call | tf_op jit(solution)/shard_map/scatter_1/pallas_call | solution.py:202
  283.6 176.3 %front_2.1 = (f32[64,4096]{1,0:T(8,128)}, bf16[2048,512]{1,0:T(8,128)(2,1)}) custom-call(f32[64,4096]{1,0:T(8,128)} %scatter_1.1.res_ref, bf16[2048,128]{1,0:T(8,128)(2,1)} %get-tuple-element.13.ids_in, f32[1,2048]{1,0:T(1,128)} %get-tuple-element.14.row_ids_in, f32[2,4096]{1,0:T(2,128)} %gain1_ref.3, f32[2,4096]{1,0:T(2,128)} %shift1_ref.3, ...), custom_call_target="tpu_custom_call" | custom-call | tf_op jit(solution)/shard_map/front_2/pallas_call | solution.py:608
  460.0 98.8 %scatter_3.1 = f32[64,4096]{1,0:T(8,128)} custom-call(bf16[2048,512]{1,0:T(8,128)(2,1)} %get-tuple-element.15.act_ref, bf16[2,512,4096]{2,1,0:T(8,128)(2,1)} %w_hbm.3, f32[64,4096]{1,0:T(8,128)} %get-tuple-element.16.res_ref, f32[2,4096]{1,0:T(2,128)} %bias_ref.7), custom_call_target="tpu_custom_call" | custom-call | tf_op jit(solution)/shard_map/scatter_3/pallas_call | solution.py:202
  558.8 2.1 convert_bitcast_fusion

commit v3 on v2

--- a/solution.py
+++ b/solution.py
@@ -9,6 +9,7 @@
 from jax.sharding import PartitionSpec as P
 
 COLS = 512
+PIECES = 2
 MESH = pl.DeviceIdType.MESH
 VMEM_LIMIT = 66 * 1000 * 1000
 
@@ -47,8 +48,8 @@
     pl.semaphore_wait(pltpu.get_barrier_semaphore(), len(others))
 
 
-def by_cols(width, fn):
-    step = min(COLS, width)
+def by_cols(width, fn, step=COLS // 2):
+    step = min(step, width)
 
     def body(n, carry):
         fn(pl.ds(pl.multiple_of(n * step, step), step))
@@ -66,13 +67,21 @@
     announce(place.neighbours())
     load_w.wait()
 
-    def remote(src, dst, slot, device):
-        return pltpu.make_async_remote_copy(src_ref=src, dst_ref=dst, send_sem=send_sem.at[slot], recv_sem=recv_sem.at[slot], device_id={"tp": device}, device_id_type=MESH)
-
-    def pair_copy(g, jj):
-        return pltpu.make_async_remote_copy(src_ref=snd.at[g % 2, jj], dst_ref=prt.at[g, jj], send_sem=pair_send.at[g, jj], recv_sem=pair_recv.at[g, jj], device_id={"tp": place.partner}, device_id_type=MESH)
-
-    def product(core, g, dst):
+    span = width // PIECES
+
+    def piece_of(z):
+        return pl.ds(z * span, span)
+
+    def by_piece(z, fn, step=COLS // 2):
+        by_cols(span, lambda at: fn(pl.ds(pl.multiple_of(z * span + at.start, 128), at.size)), step)
+
+    def remote(src, dst, slot, z, device):
+        return pltpu.make_async_remote_copy(src_ref=src.at[:, piece_of(z)], dst_ref=dst.at[:, piece_of(z)], send_sem=send_sem.at[slot, z], recv_sem=recv_sem.at[slot, z], device_id={"tp": device}, device_id_type=MESH)
+
+    def pair_copy(g, jj, z):
+        return pltpu.make_async_remote_copy(src_ref=snd.at[g % 2, jj, :, piece_of(z)], dst_ref=prt.at[g, jj, :, piece_of(z)], send_sem=pair_send.at[g, jj, z], recv_sem=pair_recv.at[g, jj, z], device_id={"tp": place.partner}, device_id_type=MESH)
+
+    def product(core, g, z, dst):
         starts = [pl.multiple_of(place.dev(i, j, core) * rows + h * half, half) for j in STEPS for h, i in enumerate((STEPS[g], OTHER_SIDE[g]))]
 
         def piece(cols):
@@ -81,7 +90,7 @@
             for jj in range(side):
                 dst[jj, :, cols] = part[jj * rows:(jj + 1) * rows]
 
-        by_cols(width, piece)
+        by_piece(z, piece, COLS)
 
     def pair_sum(g, jj, h, cols):
         at = pl.ds(h * half, half)
@@ -90,50 +99,50 @@
     far, plus, minus, here = range(side)
     sent = []
 
-    def send(src, dst, slot, device):
-        copy = remote(src, dst, slot, device)
+    def send(src, dst, slot, z, device):
+        copy = remote(src, dst, slot, z, device)
         copy.start()
         sent.append(copy)
 
-    def arrived(dst, slot):
-        remote(dst, dst, slot, place.me).wait_recv()
-
-    def open_group(g):
+    def arrived(dst, slot, z):
+        remote(dst, dst, slot, z, place.me).wait_recv()
+
+    def open_group(g, z):
         for jj in range(side):
             if g >= 2:
-                pair_copy(g - 2, jj).wait_send()
-        product(1 - place.core, g, snd.at[g % 2])
-        if g == 0:
+                pair_copy(g - 2, jj, z).wait_send()
+        product(1 - place.core, g, z, snd.at[g % 2])
+        if g == 0 and z == 0:
             meet(place.neighbours())
         for jj in range(side):
-            pair_copy(g, jj).start()
-        product(place.core, g, own.at[g])
+            pair_copy(g, jj, z).start()
+        product(place.core, g, z, own.at[g])
         shared = set()
         for k, (jj, h) in enumerate(((far, 0), (far, 1), (plus, 1), (minus, 0))):
             if jj not in shared:
                 shared.add(jj)
-                pair_copy(g, jj).wait_recv()
+                pair_copy(g, jj, z).wait_recv()
             def stage(cols, k=k, jj=jj, h=h):
                 stg[g, k, :, cols] = pair_sum(g, jj, h, cols)
-            by_cols(width, stage)
+            by_piece(z, stage)
             dst = mid.at[g, k] if k < 2 else fin.at[g, k]
             slot = 6 * g + (4 + k if k < 2 else k)
-            send(stg.at[g, k], dst, slot, place.second[1 if k % 2 == 0 else -1])
-
-    def relay(g):
+            send(stg.at[g, k], dst, slot, z, place.second[1 if k % 2 == 0 else -1])
+
+    def relay(g, z):
         for k, (jj, h) in enumerate(((plus, 0), (minus, 1))):
-            arrived(mid.at[g, k], 6 * g + 4 + k)
+            arrived(mid.at[g, k], 6 * g + 4 + k, z)
             def add(cols, k=k, jj=jj, h=h):
                 mid[g, k, :, cols] += pair_sum(g, jj, h, cols)
-            by_cols(width, add)
-            send(mid.at[g, k], fin.at[g, k], 6 * g + k, place.second[1 if k == 0 else -1])
+            by_piece(z, add)
+            send(mid.at[g, k], fin.at[g, k], 6 * g + k, z, place.second[1 if k == 0 else -1])
 
     base = 6 * side
 
-    def close_group(g):
-        pair_copy(g, here).wait_recv()
+    def close_group(g, z):
+        pair_copy(g, here, z).wait_recv()
         for k in range(4):
-            arrived(fin.at[g, k], 6 * g + k)
+            arrived(fin.at[g, k], 6 * g + k, z)
 
         def total(h, cols):
             return pair_sum(g, here, h, cols) + fin[g, 0 if h == 0 else 1, :, cols] + fin[g, 3 if h == 0 else 2, :, cols]
@@ -141,53 +150,45 @@
         def keep(k, h):
             def fn(cols):
                 stg2[k, :, cols] = total(h, cols)
-            by_cols(width, fn)
+            by_piece(z, fn)
 
         def join(k):
-            arrived(mid2.at[k], base + 4 + k)
+            arrived(mid2.at[k], base + 4 + k, z)
             def fn(cols):
                 mid2[k, :, cols] += total(k, cols)
-            by_cols(width, fn)
-            send(mid2.at[k], fin2.at[k], base + k, place.first[1 if k == 0 else -1])
+            by_piece(z, fn)
+            send(mid2.at[k], fin2.at[k], base + k, z, place.first[1 if k == 0 else -1])
 
         if g == far:
             keep(0, 0)
-            send(stg2.at[0], mid2.at[0], base + 4, place.first[1])
+            send(stg2.at[0], mid2.at[0], base + 4, z, place.first[1])
             keep(1, 1)
-            send(stg2.at[1], mid2.at[1], base + 5, place.first[-1])
+            send(stg2.at[1], mid2.at[1], base + 5, z, place.first[-1])
         elif g == plus:
             join(0)
             join(1)
         elif g == minus:
             keep(2, 1)
-            send(stg2.at[2], fin2.at[2], base + 2, place.first[1])
+            send(stg2.at[2], fin2.at[2], base + 2, z, place.first[1])
             keep(3, 0)
-            send(stg2.at[3], fin2.at[3], base + 3, place.first[-1])
+            send(stg2.at[3], fin2.at[3], base + 3, z, place.first[-1])
         else:
             for k in range(4):
-                arrived(fin2.at[k], base + k)
+                arrived(fin2.at[k], base + k, z)
             for h in range(2):
                 def fn(cols, h=h):
                     at = pl.ds(h * half, half)
                     summed = total(h, cols) + fin2[0 if h == 0 else 1, :, cols] + fin2[3 if h == 0 else 2, :, cols]
                     out_ref[at, cols] = res_ref[at, cols] + (summed + bias_ref[layer:layer + 1, cols])
-                by_cols(width, fn)
-
-    open_group(0)
-    open_group(1)
-    open_group(2)
-    relay(0)
-    open_group(3)
-    relay(1)
-    close_group(0)
-    relay(2)
-    close_group(1)
-    relay(3)
-    close_group(2)
-    close_group(3)
+                by_piece(z, fn)
+
+    for act, g in ((open_group, 0), (open_group, 1), (open_group, 2), (relay, 0), (open_group, 3), (relay, 1), (close_group, 0), (relay, 2), (close_group, 1), (relay, 3), (close_group, 2), (close_group, 3)):
+        for z in range(PIECES):
+            act(g, z)
     for g in (side - 2, side - 1):
         for jj in range(side):
-            pair_copy(g, jj).wait_send()
+            for z in range(PIECES):
+                pair_copy(g, jj, z).wait_send()
     for copy in sent:
         copy.wait_send()
 
@@ -216,10 +217,10 @@
             pltpu.VMEM((2, half, width), jnp.float32),
             pltpu.VMEM((4, half, width), jnp.float32),
             pltpu.SemaphoreType.DMA,
-            pltpu.SemaphoreType.DMA((side, side)),
-            pltpu.SemaphoreType.DMA((side, side)),
-            pltpu.SemaphoreType.DMA((6 * side + 6,)),
-            pltpu.SemaphoreType.DMA((6 * side + 6,)),
+            pltpu.SemaphoreType.DMA((side, side, PIECES)),
+            pltpu.SemaphoreType.DMA((side, side, PIECES)),
+            pltpu.SemaphoreType.DMA((6 * side + 6, PIECES)),
+            pltpu.SemaphoreType.DMA((6 * side + 6, PIECES)),
         ],
         compiler_params=pltpu.CompilerParams(collective_id=call_id, has_side_effects=True, vmem_limit_bytes=VMEM_LIMIT),
         name=f"scatter_{call_id}",
@@ -459,14 +460,43 @@
         src = o_own.at[pl.ds(pl.multiple_of(n * line, line), line)]
         send(src, obuf.at[o_slot(core, x, y)], os_send.at[k], os_recv.at[k], target(0, steps[k], 0))
 
-    def o_slots(i, h, dc=0):
-        return obuf.at[pl.ds(o_slot((core + dc) % 2, (x + i + side) % side, h * (side // 2)), side // 2)]
-
-    def o_send(i, h, step, index):
-        send(o_slots(i, h), o_slots(i, h), og_send.at[index], og_recv.at[index], at(step, 0, 0))
-
-    def o_share(k, i, h):
-        send(o_slots(i, h), o_slots(i, h), op_send.at[k], op_recv.at[k], at(0, 0, 1))
+    def o_view(k, i, dc=0):
+        return obuf.at[o_slot((core + dc) % 2, (x + i + side) % side, (y - steps[k] + side) % side)]
+
+    def o_half(k, i, h):
+        return o_view(k, i).at[pl.ds(h * (line // 2), line // 2)]
+
+    def o_send(k, i, h, step):
+        index = RING.index(((i - step + side + 1) % side - 1, h))
+        send(o_half(k, i, h), o_half(k, i, h), og_send.at[k, index], og_recv.at[k, index], at(step, 0, 0))
+
+    def o_arrived(k, i, h):
+        arrived(o_half(k, i, h), og_recv.at[k, RING.index((i, h))])
+
+    def o_share(k, i):
+        send(o_view(k, i), o_view(k, i), op_send.at[k, i % side], op_recv.at[k, i % side], at(0, 0, 1))
+
+    def o_first(k):
+        arrived(o_view(k, 0), os_recv.at[k])
+        for h in range(2):
+            o_send(k, 0, h, 1)
+            o_send(k, 0, 1 - h, -1)
+        o_share(k, 0)
+
+    def o_relay(k):
+        o_arrived(k, -1, 0)
+        o_send(k, -1, 0, 1)
+        o_arrived(k, 1, 1)
+        o_send(k, 1, 1, -1)
+
+    def o_rest(k):
+        o_arrived(k, -1, 1)
+        o_share(k, -1)
+        o_arrived(k, 1, 0)
+        o_share(k, 1)
+        for h in range(2):
+            o_arrived(k, 2, h)
+        o_share(k, 2)
 
     strip = min(block, line)
 
@@ -501,30 +531,26 @@
         attend_line(1)
         w_first(0)
         attend_line(2)
+        o_first(0)
         w_first(1)
         attend_line(3)
+        o_first(1)
         w_relay(0)
-        for k, dy in enumerate(steps):
-            arrived(obuf.at[o_slot(core, x, (y - dy + side) % side)], os_recv.at[k])
-        for h in range(2):
-            o_send(0, h, 1, RING.index((-1, h)))
-            o_send(0, 1 - h, -1, RING.index((1, 1 - h)))
+        o_first(3)
+        o_first(2)
+        o_relay(0)
         w_first(2)
-        for h in range(2):
-            o_share(h, 0, h)
+        o_relay(1)
         w_relay(1)
+        o_relay(3)
+        o_relay(2)
         w_first(3)
-        for k, (i, h) in enumerate(RING):
-            arrived(o_slots(i, h), og_recv.at[k])
-            if (i, h) == (-1, 0):
-                o_send(i, h, 1, RING.index((2, 0)))
-            if (i, h) == (1, 1):
-                o_send(i, h, -1, RING.index((2, 1)))
-            o_share(2 + k, i, h)
-            if k == 3:
-                w_relay(2)
-        for k, (i, h) in enumerate(((0, 0), (0, 1)) + RING):
-            arrived(o_slots(i, h, 1), op_recv.at[k])
+        for k in range(side):
+            o_rest(k)
+        w_relay(2)
+        for k in range(side):
+            for i in steps:
+                arrived(o_view(k, i, 1), op_recv.at[k, i % side])
 
         for part in range(parts):
             w_arrived(part, -1, 1)
@@ -628,8 +654,8 @@
             dma((parts, side, 2)), dma((parts, side, 2)),
             dma((parts, 6)), dma((parts, 6)),
             dma((side,)), dma((side,)),
-            dma((6,)), dma((6,)),
-            dma((8,)), dma((8,)),
+            dma((side, 6)), dma((side, 6)),
+            dma((side, side)), dma((side, side)),
             dma((parts, side, 2)), dma((parts, side, 2)),
         ],
         compiler_params=pltpu.CompilerParams(collective_id=call_id, has_side_effects=True, vmem_limit_bytes=VMEM_LIMIT),

time: 561 us -> 553 us (0.986)
  Pallas kernels: 557 us -> 548 us
    pallas_call x2, Pallas kernels: 197 us -> 192 us  [project_and_scatter(): pl.pallas_call(functools.partial(scatter_kernel, side, layer), out_shape=...]
where the time goes in v3:
time: 553 us; the launch traced here: 552 us
  Pallas kernels  548 us (99%)
    pallas_call x2, Pallas kernels, front(): pl.pallas_call(functools.partial(front_kernel, side, layer, first), out_s...  357 us
    pallas_call x2, Pallas kernels, project_and_scatter(): pl.pallas_call(functools.partial(scatter_kernel, side, layer), out_shape=...  192 us

profile of v3, /device:TPU:97, one launch (start us, length us, event | category | flops | bytes accessed | tf_op | source)
XLA Modules:
  0.0 552.3 jit_solution(4332527043541497629)
XLA Ops:
  0.0 0.7 convert_bitcast_fusion.1
  0.7 0.7 broadcast_in_dim.12.ids_in
  1.3 0.5 broadcast_in_dim.13.row_ids_in
  1.9 181.1 %front_0.1 = (f32[64,4096]{1,0:T(8,128)}, bf16[2048,512]{1,0:T(8,128)(2,1)}, bf16[2048,128]{1,0:T(8,128)(2,1)}, f32[1,2048]{1,0:T(1,128)}) custom-call(bf16[64,4096]{1,0:T(8,128)(2,1)} %bitcast.8, bf16[64,128]{1,0:T(8,128)(2,1)} %broadcast_in_dim.12.ids_in, f32[1,128]{1,0:T(1,128)} %broadcast_in_dim.13.row_ids_in, f32[2,4096]{1,0:T(2,128)} %gain1_ref.3, ...), custom_call_target="tpu_custom_call" | custom-call | tf_op jit(solution)/shard_map/front_0/pallas_call | solution.py:634
  183.0 96.0 %scatter_1.1.res_ref = f32[64,4096]{1,0:T(8,128)} custom-call(bf16[2048,512]{1,0:T(8,128)(2,1)} %get-tuple-element.11.act_ref, bf16[2,512,4096]{2,1,0:T(8,128)(2,1)} %w_hbm.3, f32[64,4096]{1,0:T(8,128)} %get-tuple-element.12.res_ref, f32[2,4096]{1,0:T(2,128)} %bias_ref.7), custom_call_target="tpu_custom_call" | custom-call | tf_op jit(solution)/shard_map/scatter_1/pallas_call | solution.py:203
  279.0 175.4 %front_2.1 = (f32[64,4096]{1,0:T(8,128)}, bf16[2048,512]{1,0:T(8,128)(2,1)}) custom-call(f32[64,4096]{1,0:T(8,128)} %scatter_1.1.res_ref, bf16[2048,128]{1,0:T(8,128)(2,1)} %get-tuple-element.13.ids_in, f32[1,2048]{1,0:T(1,128)} %get-tuple-element.14.row_ids_in, f32[2,4096]{1,0:T(2,128)} %gain1_ref.3, f32[2,4096]{1,0:T(2,128)} %shift1_ref.3, ...), custom_call_target="tpu_custom_call" | custom-call | tf_op jit(solution)/shard_map/front_2/pallas_call | solution.py:634
  454.4 95.9 %scatter_3.1 = f32[64,4096]{1,0:T(8,128)} custom-call(bf16[2048,512]{1,0:T(8,128)(2,1)} %get-tuple-element.15.act_ref, bf16[2,512,4096]{2,1,0:T(8,128)(2,1)} %w_hbm.3, f32[64,4096]{1,0:T(8,128)} %get-tuple-element.16.res_ref, f32[2,4096]{1,0:T(2,128)} %bias_ref.7), custom_call_target="tpu_custom_call" | custom-call | tf_op jit(solution)/shard_map/scatter_3/pallas_call | solution.py:203
  550.2 2.1 convert_bitcast_fusion

commit v4 on v3

--- a/solution.py
+++ b/solution.py
@@ -70,13 +70,17 @@
     span = width // PIECES
 
     def piece_of(z):
-        return pl.ds(z * span, span)
+        return pl.ds(pl.multiple_of(z * span, 128), span)
 
     def by_piece(z, fn, step=COLS // 2):
         by_cols(span, lambda at: fn(pl.ds(pl.multiple_of(z * span + at.start, 128), at.size)), step)
 
+    def block_of(place_in, z):
+        ref, index = place_in
+        return ref.at[(*index, slice(None), piece_of(z))]
+
     def remote(src, dst, slot, z, device):
-        return pltpu.make_async_remote_copy(src_ref=src.at[:, piece_of(z)], dst_ref=dst.at[:, piece_of(z)], send_sem=send_sem.at[slot, z], recv_sem=recv_sem.at[slot, z], device_id={"tp": device}, device_id_type=MESH)
+        return pltpu.make_async_remote_copy(src_ref=block_of(src, z), dst_ref=block_of(dst, z), send_sem=send_sem.at[slot, z], recv_sem=recv_sem.at[slot, z], device_id={"tp": device}, device_id_type=MESH)
 
     def pair_copy(g, jj, z):
         return pltpu.make_async_remote_copy(src_ref=snd.at[g % 2, jj, :, piece_of(z)], dst_ref=prt.at[g, jj, :, piece_of(z)], send_sem=pair_send.at[g, jj, z], recv_sem=pair_recv.at[g, jj, z], device_id={"tp": place.partner}, device_id_type=MESH)
@@ -100,9 +104,8 @@
     sent = []
 
     def send(src, dst, slot, z, device):
-        copy = remote(src, dst, slot, z, device)
-        copy.start()
-        sent.append(copy)
+        remote(src, dst, slot, z, device).start()
+        sent.append((src, dst, slot, device))
 
     def arrived(dst, slot, z):
         remote(dst, dst, slot, z, place.me).wait_recv()
@@ -112,8 +115,8 @@
             if g >= 2:
                 pair_copy(g - 2, jj, z).wait_send()
         product(1 - place.core, g, z, snd.at[g % 2])
-        if g == 0 and z == 0:
-            meet(place.neighbours())
+        if g == 0:
+            pl.when(z == 0)(lambda: meet(place.neighbours()))
         for jj in range(side):
             pair_copy(g, jj, z).start()
         product(place.core, g, z, own.at[g])
@@ -125,24 +128,24 @@
             def stage(cols, k=k, jj=jj, h=h):
                 stg[g, k, :, cols] = pair_sum(g, jj, h, cols)
             by_piece(z, stage)
-            dst = mid.at[g, k] if k < 2 else fin.at[g, k]
+            dst = (mid, (g, k)) if k < 2 else (fin, (g, k))
             slot = 6 * g + (4 + k if k < 2 else k)
-            send(stg.at[g, k], dst, slot, z, place.second[1 if k % 2 == 0 else -1])
+            send((stg, (g, k)), dst, slot, z, place.second[1 if k % 2 == 0 else -1])
 
     def relay(g, z):
         for k, (jj, h) in enumerate(((plus, 0), (minus, 1))):
-            arrived(mid.at[g, k], 6 * g + 4 + k, z)
+            arrived((mid, (g, k)), 6 * g + 4 + k, z)
             def add(cols, k=k, jj=jj, h=h):
                 mid[g, k, :, cols] += pair_sum(g, jj, h, cols)
             by_piece(z, add)
-            send(mid.at[g, k], fin.at[g, k], 6 * g + k, z, place.second[1 if k == 0 else -1])
+            send((mid, (g, k)), (fin, (g, k)), 6 * g + k, z, place.second[1 if k == 0 else -1])
 
     base = 6 * side
 
     def close_group(g, z):
         pair_copy(g, here, z).wait_recv()
         for k in range(4):
-            arrived(fin.at[g, k], 6 * g + k, z)
+            arrived((fin, (g, k)), 6 * g + k, z)
 
         def total(h, cols):
             return pair_sum(g, here, h, cols) + fin[g, 0 if h == 0 else 1, :, cols] + fin[g, 3 if h == 0 else 2, :, cols]
@@ -153,28 +156,28 @@
             by_piece(z, fn)
 
         def join(k):
-            arrived(mid2.at[k], base + 4 + k, z)
+            arrived((mid2, (k,)), base + 4 + k, z)
             def fn(cols):
                 mid2[k, :, cols] += total(k, cols)
             by_piece(z, fn)
-            send(mid2.at[k], fin2.at[k], base + k, z, place.first[1 if k == 0 else -1])
+            send((mid2, (k,)), (fin2, (k,)), base + k, z, place.first[1 if k == 0 else -1])
 
         if g == far:
             keep(0, 0)
-            send(stg2.at[0], mid2.at[0], base + 4, z, place.first[1])
+            send((stg2, (0,)), (mid2, (0,)), base + 4, z, place.first[1])
             keep(1, 1)
-            send(stg2.at[1], mid2.at[1], base + 5, z, place.first[-1])
+            send((stg2, (1,)), (mid2, (1,)), base + 5, z, place.first[-1])
         elif g == plus:
             join(0)
             join(1)
         elif g == minus:
             keep(2, 1)
-            send(stg2.at[2], fin2.at[2], base + 2, z, place.first[1])
+            send((stg2, (2,)), (fin2, (2,)), base + 2, z, place.first[1])
             keep(3, 0)
-            send(stg2.at[3], fin2.at[3], base + 3, z, place.first[-1])
+            send((stg2, (3,)), (fin2, (3,)), base + 3, z, place.first[-1])
         else:
             for k in range(4):
-                arrived(fin2.at[k], base + k, z)
+                arrived((fin2, (k,)), base + k, z)
             for h in range(2):
                 def fn(cols, h=h):
                     at = pl.ds(h * half, half)
@@ -183,14 +186,17 @@
                 by_piece(z, fn)
 
     for act, g in ((open_group, 0), (open_group, 1), (open_group, 2), (relay, 0), (open_group, 3), (relay, 1), (close_group, 0), (relay, 2), (close_group, 1), (relay, 3), (close_group, 2), (close_group, 3)):
-        for z in range(PIECES):
-            act(g, z)
-    for g in (side - 2, side - 1):
-        for jj in range(side):
-            for z in range(PIECES):
+        lax.fori_loop(0, PIECES, lambda z, carry: (act(g, z), carry)[1], 0)
+
+    def drain(z, carry):
+        for g in (side - 2, side - 1):
+            for jj in range(side):
                 pair_copy(g, jj, z).wait_send()
-    for copy in sent:
-        copy.wait_send()
+        for src, dst, slot, device in sent:
+            remote(src, dst, slot, z, device).wait_send()
+        return carry
+
+    lax.fori_loop(0, PIECES, drain, 0)
 
 
 def project_and_scatter(side, call_id, layer, act, weight, residual, bias):
@@ -344,8 +350,8 @@
 
 
 def attend_body(place, layer, qkv_ref, ids_ref, row_ids_ref, load_w, res_ref, bias_ref, out_ref, bufs, sems):
-    w_own, wbuf, obuf, o_own, scores, acc, rbuf = bufs
-    ws_send, ws_recv, wg_send, wg_recv, os_send, os_recv, og_send, og_recv, op_send, op_recv, back_send, back_recv = sems
+    w_own, wbuf, obuf, o_own, scores, acc, rbuf, relay = bufs
+    ws_send, ws_recv, wg_send, wg_recv, os_send, os_recv, og_send, og_recv, op_send, op_recv, back_send, back_recv, relay_send, relay_recv = sems
     side, me, core, x, y = place.side, place.me, place.core, place.x, place.y
     rows, width = res_ref.shape
     dim = w_own.shape[0]
@@ -354,11 +360,11 @@
     line = rows * 2 * side
     steps = STEPS
 
-    def at(dx, dy, dc):
+    def at(dx=0, dy=0, dc=0):
         return (((y + dy + side) % side) * side + (x + dx + side) % side) * 2 + (core + dc) % 2
 
-    peers = [at(dx, 0, dc) for dx in steps for dc in (1, 0) if (dx, dc) != (0, 0)]
-    columns = [at(0, dy, 0) for dy in steps[:3]]
+    peers = [at(dx, dc=dc) for dx in steps for dc in (1, 0) if (dx, dc) != (0, 0)]
+    columns = [at(dy=dy) for dy in steps[:3]]
     sent = []
 
     def send(src, dst, send_sem, recv_sem, device):
@@ -383,7 +389,7 @@
         for part in range(parts):
             for k, dx in enumerate(steps):
                 for dc in range(2):
-                    src = w_own.at[:, pl.ds(first_col(at(dx, 0, dc), part), cols)]
+                    src = w_own.at[:, pl.ds(first_col(at(dx, dc=dc), part), cols)]
                     send(src, wbuf.at[part, me], ws_send.at[part, k, dc], ws_recv.at[part, k, dc], target(dx, 0, dc))
 
     def w_slots(part, j, h):
@@ -396,19 +402,19 @@
     def w_first(part):
         for k, dx in enumerate(steps):
             for dc in range(2):
-                arrived(wbuf.at[part, at(-dx, 0, dc)], ws_recv.at[part, k, dc])
+                arrived(wbuf.at[part, at(-dx, dc=dc)], ws_recv.at[part, k, dc])
         for h in range(2):
-            send(w_slots(part, 0, h), w_slots(part, 0, h), *w_ring(part, -1, h), at(0, 1, 0))
-            send(w_slots(part, 0, 1 - h), w_slots(part, 0, 1 - h), *w_ring(part, 1, 1 - h), at(0, -1, 0))
+            send(w_slots(part, 0, h), w_slots(part, 0, h), *w_ring(part, -1, h), at(dy=1))
+            send(w_slots(part, 0, 1 - h), w_slots(part, 0, 1 - h), *w_ring(part, 1, 1 - h), at(dy=-1))
 
     def w_arrived(part, j, h):
         arrived(w_slots(part, j, h), w_ring(part, j, h)[1])
 
     def w_relay(part):
         w_arrived(part, -1, 0)
-        send(w_slots(part, -1, 0), w_slots(part, -1, 0), *w_ring(part, 2, 0), at(0, 1, 0))
+        send(w_slots(part, -1, 0), w_slots(part, -1, 0), *w_ring(part, 2, 0), at(dy=1))
         w_arrived(part, 1, 1)
-        send(w_slots(part, 1, 1), w_slots(part, 1, 1), *w_ring(part, 2, 1), at(0, -1, 0))
+        send(w_slots(part, 1, 1), w_slots(part, 1, 1), *w_ring(part, 2, 1), at(dy=-1))
 
     block = scores.shape[0]
     half = block // 2
@@ -468,13 +474,13 @@
 
     def o_send(k, i, h, step):
         index = RING.index(((i - step + side + 1) % side - 1, h))
-        send(o_half(k, i, h), o_half(k, i, h), og_send.at[k, index], og_recv.at[k, index], at(step, 0, 0))
+        send(o_half(k, i, h), o_half(k, i, h), og_send.at[k, index], og_recv.at[k, index], at(step))
 
     def o_arrived(k, i, h):
         arrived(o_half(k, i, h), og_recv.at[k, RING.index((i, h))])
 
     def o_share(k, i):
-        send(o_view(k, i), o_view(k, i), op_send.at[k, i % side], op_recv.at[k, i % side], at(0, 0, 1))
+        send(o_view(k, i), o_view(k, i), op_send.at[k, i % side], op_recv.at[k, i % side], at(dc=1))
 
     def o_first(k):
         arrived(o_view(k, 0), os_recv.at[k])
@@ -525,6 +531,11 @@
 
     def finish(at_cols):
         out_ref[:, at_cols] = res_ref[:, at_cols].astype(jnp.float32) + (rbuf[:, at_cols] + bias_ref[layer:layer + 1, at_cols])
+
+    def pass_on(part):
+        arrived(relay.at[part], relay_recv.at[part])
+        far = steps.index(2)
+        send(relay.at[part], rbuf.at[:, pl.ds(first_col(at(1), part), cols)], back_send.at[part, far, 1], back_recv.at[part, far, 1], at(-1, dc=1))
 
     def proceed():
         attend_line(0)
@@ -561,15 +572,21 @@
             project(part, True)
             for k, dx in enumerate(steps):
                 for dc in range(2):
-                    src = acc.at[part, back_rows(at(dx, 0, dc))]
+                    src = acc.at[part, back_rows(at(dx, dc=dc))]
                     dst = rbuf.at[:, pl.ds(first_col(me, part), cols)]
-                    send(src, dst, back_send.at[part, k, dc], back_recv.at[part, k, dc], target(dx, 0, dc))
+                    if dx == 2 and dc:
+                        send(src, relay.at[part], relay_send.at[part], relay_recv.at[part], at(-1))
+                    else:
+                        send(src, dst, back_send.at[part, k, dc], back_recv.at[part, k, dc], target(dx, 0, dc))
             if part == 0:
                 w_relay(3)
+            else:
+                pass_on(part - 1)
+        pass_on(parts - 1)
         for part in range(parts):
             for k, dx in enumerate(steps):
                 for dc in range(2):
-                    arrived(rbuf.at[:, pl.ds(first_col(at(-dx, 0, dc), part), cols)], back_recv.at[part, k, dc])
+                    arrived(rbuf.at[:, pl.ds(first_col(at(-dx, dc=dc), part), cols)], back_recv.at[part, k, dc])
         by_cols(width, finish)
 
     def drain():
@@ -585,7 +602,7 @@
     if first:
         ids_ref, row_ids_ref, refs = refs[0], refs[1], refs[2:]
     w_qkv_ref, w_up_ref, qkv_ref, buf1, buf2, refs = *refs[:5], refs[5:]
-    bufs, w_sem, refs = refs[:7], refs[7], refs[8:]
+    bufs, w_sem, refs = refs[:8], refs[8], refs[9:]
     sems1, sems2, sems = refs[:4], refs[4:8], refs[8:]
     thirds = w_qkv.shape[1]
     each = w_qkv.shape[4]
@@ -649,6 +666,7 @@
             pltpu.VMEM((block, seq), jnp.float32),
             pltpu.VMEM((parts, line, cols), jnp.float32),
             pltpu.VMEM((rows, width), jnp.float32),
+            pltpu.VMEM((parts, rows, cols), jnp.float32),
             dma((w_qkv.shape[1] + 2,)),
             *gather_sems, *gather_sems,
             dma((parts, side, 2)), dma((parts, side, 2)),
@@ -657,6 +675,7 @@
             dma((side, 6)), dma((side, 6)),
             dma((side, side)), dma((side, side)),
             dma((parts, side, 2)), dma((parts, side, 2)),
+            dma((parts,)), dma((parts,)),
         ],
         compiler_params=pltpu.CompilerParams(collective_id=call_id, has_side_effects=True, vmem_limit_bytes=VMEM_LIMIT),
         name=f"front_{call_id}",

time: 553 us -> 557 us (level)
  no operation moved by 1% of the time
where the time goes in v4:
time: 557 us
  Pallas kernels  553 us (99%)
    pallas_call x2, Pallas kernels, front(): pl.pallas_call(functools.partial(front_kernel, side, layer, first), out_s...  361 us
    pallas_call x2, Pallas kernels, project_and_scatter(): pl.pallas_call(functools.partial(scatter_kernel, side, layer), out_shape=...  192 us

profile of v4, /device:TPU:97, one launch (start us, length us, event | category | flops | bytes accessed | tf_op | source)
XLA Modules:
  0.0 556.8 jit_solution(17038944111136473407)
XLA Ops:
  0.0 0.7 convert_bitcast_fusion.1
  0.7 0.7 broadcast_in_dim.12.ids_in
  1.3 0.5 broadcast_in_dim.13.row_ids_in
  1.9 183.7 %front_0.1 = (f32[64,4096]{1,0:T(8,128)}, bf16[2048,512]{1,0:T(8,128)(2,1)}, bf16[2048,128]{1,0:T(8,128)(2,1)}, f32[1,2048]{1,0:T(1,128)}) custom-call(bf16[64,4096]{1,0:T(8,128)(2,1)} %bitcast.8, bf16[64,128]{1,0:T(8,128)(2,1)} %broadcast_in_dim.12.ids_in, f32[1,128]{1,0:T(1,128)} %broadcast_in_dim.13.row_ids_in, f32[2,4096]{1,0:T(2,128)} %gain1_ref.3, ...), custom_call_target="tpu_custom_call" | custom-call | tf_op jit(solution)/shard_map/front_0/pallas_call | solution.py:651
  185.5 95.7 %scatter_1.1.res_ref = f32[64,4096]{1,0:T(8,128)} custom-call(bf16[2048,512]{1,0:T(8,128)(2,1)} %get-tuple-element.11.act_ref, bf16[2,512,4096]{2,1,0:T(8,128)(2,1)} %w_hbm.3, f32[64,4096]{1,0:T(8,128)} %get-tuple-element.12.res_ref, f32[2,4096]{1,0:T(2,128)} %bias_ref.7), custom_call_target="tpu_custom_call" | custom-call | tf_op jit(solution)/shard_map/scatter_1/pallas_call | solution.py:209
  281.2 177.4 %front_2.1 = (f32[64,4096]{1,0:T(8,128)}, bf16[2048,512]{1,0:T(8,128)(2,1)}) custom-call(f32[64,4096]{1,0:T(8,128)} %scatter_1.1.res_ref, bf16[2048,128]{1,0:T(8,128)(2,1)} %get-tuple-element.13.ids_in, f32[1,2048]{1,0:T(1,128)} %get-tuple-element.14.row_ids_in, f32[2,4096]{1,0:T(2,128)} %gain1_ref.3, f32[2,4096]{1,0:T(2,128)} %shift1_ref.3, ...), custom_call_target="tpu_custom_call" | custom-call | tf_op jit(solution)/shard_map/front_2/pallas_call | solution.py:651
  458.6 96.1 %scatter_3.1 = f32[64,4096]{1,0:T(8,128)} custom-call(bf16[2048,512]{1,0:T(8,128)(2,1)} %get-tuple-element.15.act_ref, bf16[2,512,4096]{2,1,0:T(8,128)(2,1)} %w_hbm.3, f32[64,4096]{1,0:T(8,128)} %get-tuple-element.16.res_ref, f32[2,4096]{1,0:T(2,128)} %bias_ref.7), custom_call_target="tpu_custom_call" | custom-call | tf_op jit(solution)/shard_map/scatter_3/pallas_call | solution.py:209
  554.8 2.1 convert_bitcast_fusion
